TPU v7x, 512 devices: a 8x2x16 block of a 8x8x16 slice. The times are simulated.
512 devices in a mesh: members: 2 (over y), band: 32 (over z, core), head: 8 (over x).
Axes of the slice: x: 8, y: 2, z: 16, core: 2. Of those that a mesh axis runs over, the one named last changes fastest.
The devices are a block of a 8x8x16 slice.
Arguments:
- grid_feats: bfloat16 [32768, 1024], P(('members', 'band')), parts along dimension 0, may hold values from -6 to 6
- mesh_feats: bfloat16 [32768, 1024], P(('members', 'band')), parts along dimension 0, may hold values from -6 to 6
- enc_in: bfloat16 [3, 1024, 1024], P(None, 'band', 'head'), may hold values from -0.19921875 to 0.19921875
- enc_out: bfloat16 [1024, 1024], P('head', 'band'), may hold values from -0.1875 to 0.1875
- proc_in: bfloat16 [3, 1024, 1024], P(None, 'band', 'head'), may hold values from -0.19921875 to 0.19921875
- proc_out: bfloat16 [1024, 1024], P('head', 'band'), may hold values from -0.1875 to 0.1875
- ff_up: bfloat16 [1024, 4096], P('band', 'head'), may hold values from -0.1875 to 0.1875
- ff_down: bfloat16 [4096, 1024], P('head', 'band'), may hold values from -0.09375 to 0.09375
- dec_in: bfloat16 [3, 1024, 1024], P(None, 'band', 'head'), may hold values from -0.19921875 to 0.19921875
- dec_out: bfloat16 [1024, 1024], P('head', 'band'), may hold values from -0.1875 to 0.1875
- enc_list: int32 [128, 8], replicated, may hold values from 0 to 127, as said below
- enc_count: int32 [128], replicated, may hold values from 1 to 8
- dec_list: int32 [128, 8], replicated, may hold values from 0 to 127, as said below
- dec_count: int32 [128], replicated, may hold values from 1 to 8
- window_ids: int32 [16384], replicated, may hold values from 0 to 20, never falling along the last dimension, each value on 1 to 1536 neighbouring positions
Outputs:
- grid_out: bfloat16 [32768, 1024], P(('members', 'band', 'head')), parts along dimension 0
There are 2 independent parts, one for each index of `members`. A program takes and returns all parts, laid end to end along the dimension named above; an argument that names none is the same for every part. Nothing has to cross between parts.
Inputs may be any that keep to these rules, and one draw needn't show every extreme that they name: `enc_list`: each row holds distinct block numbers. Every block listed for mesh block m lies in the band of 512 grid points with the same band number as m's band of 512 nodes, or in the band just before or just after it. Only the first enc_count[m] slots of row m of enc_list are used. `dec_list`: each row holds distinct block numbers. Every block listed for grid block g lies in the band of 512 mesh nodes with the same band number as g's band of 512 grid points, or in the band just before or just after it. Only the first dec_count[g] slots of row g of dec_list are used. `window_ids`: never falls along the nodes; each window holds at most 1536 consecutive nodes.
All inputs are finite; a program needn't handle non-finite values.
Results may differ from a plain program's by a relative error of at most 0.02.
Values may be sent and summed in bfloat16 or wider, within the bound.
A program may use at most 64 MiB of HBM per device.

v0:
```python
import jax
import jax.numpy as jnp
from jax import lax
from jax.sharding import Mesh
from jax.sharding import PartitionSpec as P

HD = 64
BLOCK = 128
WINDOW = 1536
BAND = ("band_0", "band_1")
MEMBERS_BAND = ("members", "band_0", "band_1")
MEMBERS_BAND_HEAD = ("members", "band_0", "band_1", "head")


EPSILON = 1e-05
NEGATIVE = -1e30


def joined_along(blocks, dim):
    dims = list(blocks.shape[1:])
    dims[dim] *= blocks.shape[0]
    return jnp.moveaxis(blocks, 0, dim).reshape(dims)


def all_blocks(array, axes, order):
    blocks = array[None]
    for k in order:
        blocks = lax.all_gather(blocks, axes[k], axis=0, tiled=True)
    block = [lax.axis_size(axes[k]) for k in reversed(order)]
    blocks = blocks.reshape(*block, *array.shape)
    turned = sorted(range(len(order)), key=lambda place: order[len(order) - 1 - place])
    return blocks.transpose(*turned, *range(len(order), blocks.ndim)).reshape(-1, *array.shape)


def whole_of(array, axes, order, dim):
    return joined_along(all_blocks(array, axes, order), dim)


def padded(block, sides, width):
    for axis, dim in sides:
        count = lax.axis_size(axis)
        forward = [(i, i + 1) for i in range(count - 1)]
        backward = [(target, source) for source, target in forward]
        low = lax.ppermute(
            lax.slice_in_dim(block, block.shape[dim] - width, None, axis=dim), axis, forward
        )
        high = lax.ppermute(lax.slice_in_dim(block, 0, width, axis=dim), axis, backward)
        block = jnp.concatenate([low, block, high], axis=dim)
    return block


def copy_for_each(array, axis):
    size = lax.axis_size(axis)
    return lax.all_to_all(
        jnp.broadcast_to(array[None], (size, *array.shape)), axis, 0, 0, tiled=True
    )


def gathered_copies(array, axis, dim):
    return joined_along(copy_for_each(array, axis), dim)


def shifted(block, axis, distance):
    devices = range(lax.axis_size(axis))
    route = [(i - distance, i) for i in devices if i - distance in devices]
    return lax.ppermute(block, axis, route)


def split_up(array, dim, size):
    dims = array.shape
    blocks = array.reshape(*dims[:dim], size, dims[dim] // size, *dims[dim + 1 :])
    return jnp.moveaxis(blocks, dim, 0)


def summed_on_arrival(array, axis, dim):
    size = lax.axis_size(axis)
    blocks = lax.all_to_all(split_up(array, dim, size), axis, 0, 0, tiled=True)
    return jnp.sum(blocks.astype(jnp.float32), axis=0)


def normed(source):
    values_f = source.astype(jnp.float32)
    centred = values_f - jnp.mean(values_f, axis=-1, keepdims=True)
    variance = jnp.mean(centred * centred, axis=-1, keepdims=True)
    return (centred * lax.rsqrt(variance + EPSILON)).astype(jnp.bfloat16)


def fold_three(sources, carry, piece):
    width = piece.shape[1]
    return tuple(
        (
            total
            + jnp.dot(
                lax.slice_in_dim(source, 0, width, axis=1),
                piece[which],
                preferred_element_type=jnp.float32,
            )
            for which, (total, source) in enumerate(zip(carry, sources))
        )
    )


def fold_rows(source, total, piece):
    return total + jnp.dot(
        lax.slice_in_dim(source, 0, piece.shape[0], axis=1),
        piece,
        preferred_element_type=jnp.float32,
    )


def columns_of(source, piece):
    return jnp.dot(source, piece, preferred_element_type=jnp.float32)


def head_scores(queries, key_rows, head_index, allowed):
    lower = head_index * HD
    scores = jnp.einsum(
        "qd,kd->qk",
        queries[:, lower : lower + HD],
        key_rows[:, lower : lower + HD],
        preferred_element_type=jnp.float32,
    ) * HD ** (-0.5)
    scores = jnp.where(allowed, scores, NEGATIVE)
    maxima = jnp.max(scores, axis=1, keepdims=True)
    expo = jnp.where(allowed, jnp.exp(scores - maxima), 0.0)
    return (expo, maxima, jnp.sum(expo, axis=1, keepdims=True))


def attend_rounded(queries, key_rows, value_rows, allowed):
    outputs = []
    for head_index in range(queries.shape[1] // HD):
        expo, maxima, totals = head_scores(queries, key_rows, head_index, allowed)
        weights = (expo / totals).astype(jnp.bfloat16)
        lower = head_index * HD
        outputs.append(
            jnp.dot(weights, value_rows[:, lower : lower + HD], preferred_element_type=jnp.float32)
        )
    return jnp.concatenate(outputs, axis=1).astype(jnp.bfloat16)


def partial_attend(queries, key_rows, value_rows, allowed):
    outputs, maxima_all, totals_all = ([], [], [])
    for head_index in range(queries.shape[1] // HD):
        expo, maxima, totals = head_scores(queries, key_rows, head_index, allowed)
        lower = head_index * HD
        outputs.append(jnp.dot(expo, value_rows[:, lower : lower + HD].astype(jnp.float32)))
        maxima_all.append(maxima)
        totals_all.append(totals)
    return (
        jnp.concatenate(outputs, axis=1),
        jnp.concatenate(maxima_all, axis=1),
        jnp.concatenate(totals_all, axis=1),
    )


def listed_attend(queries, key_pool, value_pool, lists, counts, base_block, rounded):
    width = queries.shape[1]
    rows = queries.shape[0]
    pool_blocks = key_pool.shape[0] // BLOCK
    key_blocks = key_pool.reshape(pool_blocks, BLOCK, width)
    value_blocks = value_pool.reshape(pool_blocks, BLOCK, width)
    slots = lists.shape[1]

    def one_block(index):
        listed = lists[index] - base_block
        inside = (
            (listed >= 0)
            & (listed < pool_blocks)
            & (jnp.arange(slots, dtype=jnp.int32) < counts[index])
        )
        safe = jnp.clip(listed, 0, pool_blocks - 1)
        block_keys = key_blocks[safe].reshape(slots * BLOCK, width)
        block_values = value_blocks[safe].reshape(slots * BLOCK, width)
        allowed = jnp.repeat(inside, BLOCK)[None, :]
        block_queries = lax.dynamic_slice_in_dim(queries, index * BLOCK, BLOCK, 0)
        if rounded:
            return attend_rounded(block_queries, block_keys, block_values, allowed)
        return partial_attend(block_queries, block_keys, block_values, allowed)

    result = lax.map(one_block, jnp.arange(rows // BLOCK, dtype=jnp.int32))
    return jax.tree.map(lambda stacked: stacked.reshape(rows, stacked.shape[-1]), result)


def normalize(outputs, totals):
    rows = outputs.shape[0]
    heads_here = totals.shape[1]
    shaped = outputs.reshape(rows, heads_here, HD) / totals[:, :, None]
    return shaped.reshape(rows, heads_here * HD).astype(jnp.bfloat16)


def per_device(
    grid_feats,
    mesh_feats,
    enc_in,
    enc_out,
    proc_in,
    proc_out,
    ff_up,
    ff_down,
    dec_in,
    dec_out,
    enc_list,
    enc_count,
    dec_list,
    dec_count,
    window_ids,
):
    band_index = lax.axis_index(BAND)
    grid_rows = grid_feats.shape[0]
    mesh_rows = mesh_feats.shape[0]
    width = enc_in.shape[2]
    grid_blocks = grid_rows // BLOCK
    mesh_blocks = mesh_rows // BLOCK
    grid_norm = normed(grid_feats)
    mesh_norm = normed(mesh_feats)
    grid_zeros = jnp.zeros((grid_rows, width), jnp.float32)
    mesh_zeros = jnp.zeros((mesh_rows, width), jnp.float32)
    enc_q, enc_k, enc_v = fold_three(
        (mesh_norm, grid_norm, grid_norm),
        (mesh_zeros, grid_zeros, grid_zeros),
        whole_of(enc_in, BAND, (0, 1), 1),
    )
    enc_q = enc_q.astype(jnp.bfloat16)
    enc_k = enc_k.astype(jnp.bfloat16)
    enc_v = enc_v.astype(jnp.bfloat16)
    my_lists = lax.dynamic_slice_in_dim(enc_list, band_index * mesh_blocks, mesh_blocks, 0)
    my_counts = lax.dynamic_slice_in_dim(enc_count, band_index * mesh_blocks, mesh_blocks, 0)
    pool = padded(jnp.stack([enc_k, enc_v]), ((BAND, 1),), grid_rows)
    outputs, maxima, totals = listed_attend(
        enc_q, pool[0], pool[1], my_lists, my_counts, (band_index - 1) * grid_blocks, False
    )
    enc_attn = normalize(outputs, totals)
    enc_terms = columns_of(enc_attn, gathered_copies(enc_out, BAND, 1))
    mesh_state = mesh_feats.astype(jnp.float32) + lax.psum(
        enc_terms.astype(jnp.bfloat16), "head"
    ).astype(jnp.float32)
    proc_norm = normed(mesh_state)
    proc_q, proc_k, proc_v = fold_three(
        (proc_norm, proc_norm, proc_norm),
        (mesh_zeros, mesh_zeros, mesh_zeros),
        whole_of(proc_in, BAND, (0, 1), 1),
    )
    proc_q = proc_q.astype(jnp.bfloat16)
    pairs = jnp.stack([proc_k.astype(jnp.bfloat16), proc_v.astype(jnp.bfloat16)])
    reach = (WINDOW + mesh_rows - 2) // mesh_rows
    slab_parts = {0: pairs}
    for distance in range(1, reach + 1):
        for direction in (1, -1):
            slab_parts[direction * distance] = shifted(pairs, BAND, -direction * distance)
    slab = jnp.concatenate([slab_parts[offset] for offset in range(-reach, reach + 1)], axis=1)
    padded_ids = jnp.pad(window_ids, (reach * mesh_rows, reach * mesh_rows), constant_values=-1)
    slab_ids = lax.dynamic_slice_in_dim(
        padded_ids, band_index * mesh_rows, (2 * reach + 1) * mesh_rows, 0
    )
    slab_start = (band_index - reach) * mesh_rows
    span = 2 * WINDOW

    def window_block(index):
        first = band_index * mesh_rows + index * BLOCK
        first_id = window_ids[first]
        window_start = jnp.sum((window_ids < first_id).astype(jnp.int32))
        local = window_start - slab_start
        block_keys = lax.dynamic_slice_in_dim(slab[0], local, span, 0)
        block_values = lax.dynamic_slice_in_dim(slab[1], local, span, 0)
        key_ids = lax.dynamic_slice_in_dim(slab_ids, local, span, 0)
        query_ids = lax.dynamic_slice_in_dim(window_ids, first, BLOCK, 0)
        block_queries = lax.dynamic_slice_in_dim(proc_q, index * BLOCK, BLOCK, 0)
        return attend_rounded(
            block_queries, block_keys, block_values, query_ids[:, None] == key_ids[None, :]
        )

    proc_attn = lax.map(window_block, jnp.arange(mesh_blocks, dtype=jnp.int32)).reshape(
        mesh_rows, width
    )
    proc_terms = columns_of(proc_attn, gathered_copies(proc_out, BAND, 1))
    mesh_mid = mesh_state + lax.psum(proc_terms.astype(jnp.bfloat16), "head").astype(jnp.float32)
    ff_norm = normed(mesh_mid)
    hidden = fold_rows(
        ff_norm,
        jnp.zeros((mesh_rows, ff_up.shape[1]), jnp.float32),
        whole_of(ff_up, BAND, (0, 1), 0),
    )
    hidden = jax.nn.gelu(hidden, approximate=False).astype(jnp.bfloat16)
    ff_terms = columns_of(hidden, whole_of(ff_down, BAND, (0, 1), 1))
    mesh_final = mesh_mid + lax.psum(ff_terms.astype(jnp.bfloat16), "head").astype(jnp.float32)
    final_norm = normed(mesh_final)
    dec_q, dec_k, dec_v = fold_three(
        (grid_norm, final_norm, final_norm),
        (grid_zeros, mesh_zeros, mesh_zeros),
        whole_of(dec_in, BAND, (0, 1), 1),
    )
    dec_q = dec_q.astype(jnp.bfloat16)
    dec_pool = padded(
        jnp.stack([dec_k.astype(jnp.bfloat16), dec_v.astype(jnp.bfloat16)]), ((BAND, 1),), mesh_rows
    )
    grid_lists = lax.dynamic_slice_in_dim(dec_list, band_index * grid_blocks, grid_blocks, 0)
    grid_counts = lax.dynamic_slice_in_dim(dec_count, band_index * grid_blocks, grid_blocks, 0)
    dec_attn = listed_attend(
        dec_q,
        dec_pool[0],
        dec_pool[1],
        grid_lists,
        grid_counts,
        (band_index - 1) * mesh_blocks,
        True,
    )
    full_out = gathered_copies(dec_out, BAND, 1)
    share = grid_rows // lax.axis_size("head")
    summed = summed_on_arrival(
        jnp.dot(
            lax.slice_in_dim(dec_attn, 0, share * lax.axis_size("head"), axis=0),
            full_out,
            preferred_element_type=jnp.float32,
        ).astype(jnp.bfloat16),
        "head",
        0,
    )
    residual = lax.dynamic_slice_in_dim(
        grid_feats, lax.axis_index("head") * share, share, 0
    ).astype(jnp.float32)
    return (residual + summed).astype(jnp.bfloat16)


def solution(mesh):
    finer = Mesh(
        mesh.devices.reshape(mesh.shape["members"], 16, 2, mesh.shape["head"]),
        ("members", "band_0", "band_1", "head"),
    )
    placed = (
        P(MEMBERS_BAND, None),
        P(MEMBERS_BAND, None),
        P(None, BAND, "head"),
        P("head", BAND),
        P(None, BAND, "head"),
        P("head", BAND),
        P(BAND, "head"),
        P("head", BAND),
        P(None, BAND, "head"),
        P("head", BAND),
        P(),
        P(),
        P(),
        P(),
        P(),
    )
    return jax.shard_map(
        per_device,
        mesh=finer,
        in_specs=placed,
        out_specs=P(MEMBERS_BAND_HEAD, None),
        check_vma=False,
    )
```

profile of v0, /device:TPU:65, one launch (start us, length us, event | category | flops | bytes accessed | tf_op | source)
XLA Modules:
  0.0 632.4 jit_solution(11155338328643831637)
XLA Ops:
  7.4 1.5 convert_reduce_fusion.2
  8.9 1.6 fusion.64
  10.9 64.3 %all-gather.1 = bf16[48,32,128]{2,1,0:T(8,128)(2,1)S(1)} all-gather(bf16[3,32,128]{2,1,0:T(8,128)(2,1)S(1)} %copy-done.15), channel_id=3, replica_groups=mesh['members'=2,'band_0'=16,'band_1'=2,'head'=8] {'band_0'}, dimensions={0}, use_global_device_ids=true | all-gather | bytes 417792 | tf_op jit(solution)/shard_map/all_gather | solution.py:28
  75.2 9.4 %all_gather.33 = bf16[32,3,32,128]{3,2,1,0:T(8,128)(2,1)S(1)} all-gather(bf16[16,3,32,128]{3,2,1,0:T(8,128)(2,1)S(1)} %bitcast.225), channel_id=1, replica_groups=mesh['members'=2,'band_0'=16,'band_1'=2,'head'=8] {'band_1'}, dimensions={0}, use_global_device_ids=true | all-gather | bytes 1179648 | tf_op jit(solution)/shard_map/all_gather | solution.py:28
  85.8 2.3 collective-permute-start.1
  88.1 3.3 collective-permute-start
  92.2 4.8 all-to-all-start
  100.3 39.7 %while.34 = (s32[]{:T(128)}, f32[4,128,128]{2,1,0:T(8,128)}, f32[4,128,2]{1,2,0:T(2,128)}, s32[4]{0:T(128)}, s32[4,8]{1,0:T(4,128)S(1)}, /*index=5*/s32[]{:T(128...) while((s32[]{:T(128)}, f32[4,128,128]{2,1,0:T(8,128)}, ...), condition=%wide.region_9.10_spmd, body=%wide.region_4.9_spmd.sunk | while | flops 69223264 | bytes 5784073 | solution.py:180
  100.3 1.2 dynamic_slice.119
  104.6 1.2 dynamic_slice.120
  114.5 1.2 dynamic_slice.120
  124.5 1.2 dynamic_slice.120
  134.4 1.2 dynamic_slice.120
  142.0 2.4 convolution_convert_fusion.6
  144.5 24.8 %all-gather.4 = bf16[8192,32]{0,1:T(8,128)(2,1)S(1)} all-gather(bf16[512,32]{0,1:T(8,128)(2,1)S(1)} %copy-done.13), channel_id=6, replica_groups=mesh['members'=2,'band_0'=16,'band_1'=2,'head'=8] {'band_0'}, dimensions={0}, use_global_device_ids=true | all-gather | bytes 557056 | tf_op jit(solution)/shard_map/all_gather | solution.py:28
  171.1 16.2 %all-to-all-start.1 = ((bf16[32,128,32]{1,2,0:T(8,128)(2,1)}), bf16[32,128,32]{1,2,0:T(8,128)(2,1)S(1)}, u32[]{:S(2)}, u32[]{:S(2)}) async-start(bf16[32,128,32]{1,2,0:T(8,128)(2,1)} %broadcast_in_dim.159), calls=%async_computation.1 | async-start | bytes 524288 | tf_op jit(solution)/shard_map/all_to_all | solution.py:54
  187.4 37.6 %all-gather.3 = bf16[512,512]{1,0:T(8,128)(2,1)} all-gather(bf16[32,512]{1,0:T(8,128)(2,1)S(1)} %copy-done.14), channel_id=5, replica_groups=mesh['members'=2,'band_0'=16,'band_1'=2,'head'=8] {'band_0'}, dimensions={0}, use_global_device_ids=true | all-gather | bytes 557056 | tf_op jit(solution)/shard_map/all_gather | solution.py:28
  225.1 23.3 %all-gather.2 = bf16[48,32,128]{2,1,0:T(8,128)(2,1)S(1)} all-gather(bf16[3,32,128]{2,1,0:T(8,128)(2,1)S(1)} %copy-done.16), channel_id=4, replica_groups=mesh['members'=2,'band_0'=16,'band_1'=2,'head'=8] {'band_0'}, dimensions={0}, use_global_device_ids=true | all-gather | bytes 417792 | tf_op jit(solution)/shard_map/all_gather | solution.py:28
  248.4 13.6 %all_gather.35 = bf16[32,3,32,128]{3,2,1,0:T(8,128)(2,1)S(1)} all-gather(bf16[16,3,32,128]{3,2,1,0:T(8,128)(2,1)S(1)} %bitcast.226), channel_id=1, replica_groups=mesh['members'=2,'band_0'=16,'band_1'=2,'head'=8] {'band_1'}, dimensions={0}, use_global_device_ids=true | all-gather | bytes 1179648 | tf_op jit(solution)/shard_map/all_gather | solution.py:28
  262.2 1.7 fusion.66
  265.8 4.0 collective-permute-start.2
  269.9 3.3 collective-permute-start.3
  273.2 2.5 collective-permute-start.4
  275.7 2.0 collective-permute-start.5
  277.7 1.3 collective-permute-start.6
  279.4 1.3 collective-permute-start.7
  281.8 1.9 collective-permute-done.4
  284.9 3.0 collective-permute-done.6
  288.0 10.1 %collective-permute-done.7 = bf16[2,512,128]{2,1,0:T(8,128)(2,1)S(1)} collective-permute-done((bf16[2,512,128]{2,1,0:T(8,128)(2,1)S(1)}, bf16[2,512,128]{2,1,0:T(8,128)(2,1)S(1)}, u32[]{:S(2)}, u32[]{:S(2)}) %collective-permute-start.7) | collective-permute-done | bytes 262176 | tf_op jit(solution)/shard_map/ppermute | solution.py:66
  299.4 49.0 %while.35 = (s32[]{:T(128)}, bf16[4,128,128]{2,1,0:T(8,128)(2,1)S(1)}, s32[4]{0:T(128)S(1)}, s32[]{:T(128)}, s32[16384]{0:T(1024)S(1)}, /*index=5*/s32[]{:T(128)...) while((s32[]{:T(128)}, ...), condition=%wide.region_19.20_spmd, body=%wide.region_13.19_spmd.sunk | while | flops 211287568 | bytes 26145704 | solution.py:272
  299.4 1.6 fusion.224
  302.8 1.3 convert_reduce_fusion.5
  304.7 1.6 dynamic-slice_bitcast_fusion.3
  306.5 1.8 fusion.225
  311.6 1.6 fusion.224
  315.1 1.3 convert_reduce_fusion.5
  317.0 1.6 dynamic-slice_bitcast_fusion.3
  318.7 1.8 fusion.225
  323.9 1.6 fusion.224
  327.3 1.3 convert_reduce_fusion.5
  329.3 1.6 dynamic-slice_bitcast_fusion.3
  331.0 1.8 fusion.225
  336.1 1.6 fusion.224
  339.6 1.3 convert_reduce_fusion.5
  341.5 1.6 dynamic-slice_bitcast_fusion.3
  343.3 1.8 fusion.225
  348.4 1.4 convolution_convert_fusion.5
  350.2 2.8 copy.72
  353.0 2.3 copy.70
  355.3 77.1 %all-reduce.7.cloned.1.call-done = bf16[512,1024]{1,0:T(8,128)(2,1)} async-done(((bf16[512,1024]{1,0:T(8,128)(2,1)}), bf16[512,1024]{1,0:T(8,128)(2,1)}) %all-reduce.7.cloned.1.call-update) | async-done | bytes 1048592 | tf_op jit(solution)/shard_map/psum | solution.py:276
  432.5 2.0 fusion.150
  435.7 5.6 convolution_convert_fusion.7
  441.4 26.9 %all-gather = bf16[48,32,128]{2,1,0:T(8,128)(2,1)S(1)} all-gather(bf16[3,32,128]{2,1,0:T(8,128)(2,1)S(1)} %copy-done.17), channel_id=2, replica_groups=mesh['members'=2,'band_0'=16,'band_1'=2,'head'=8] {'band_0'}, dimensions={0}, use_global_device_ids=true | all-gather | bytes 417792 | tf_op jit(solution)/shard_map/all_gather | solution.py:28
  468.3 14.2 %all_gather.31 = bf16[32,3,32,128]{3,2,1,0:T(8,128)(2,1)S(1)} all-gather(bf16[16,3,32,128]{3,2,1,0:T(8,128)(2,1)S(1)} %bitcast.227), channel_id=1, replica_groups=mesh['members'=2,'band_0'=16,'band_1'=2,'head'=8] {'band_1'}, dimensions={0}, use_global_device_ids=true | all-gather | bytes 1179648 | tf_op jit(solution)/shard_map/all_gather | solution.py:28
  483.4 45.9 %all-reduce.9.cloned.1.call-done = bf16[512,1024]{1,0:T(8,128)(2,1)} async-done(((bf16[512,1024]{1,0:T(8,128)(2,1)}), bf16[512,1024]{1,0:T(8,128)(2,1)}) %all-reduce.9.cloned.1.call-update) | async-done | bytes 1048592 | tf_op jit(solution)/shard_map/psum | solution.py:285
  529.3 1.6 fusion.89
  533.3 7.6 %collective-permute-start.9 = (bf16[2,512,128]{2,1,0:T(8,128)(2,1)S(1)}, bf16[2,512,128]{2,1,0:T(8,128)(2,1)S(1)}, u32[]{:S(2)}, u32[]{:S(2)}) collective-permute-start(bf16[2,512,128]{2,1,0:T(8,128)(2,1)S(1)} %pad_maximum_fusion.6), channel_id=1, source_target_pairs={{8,0},{16,8},{24,16},{32,24},{40,32},{48,40},{56,48},{64,56},{72,6... | collective-permute-start | bytes 786440 | tf_op jit(solution)/shard_map/ppermute | solution.py:47
  540.9 3.2 collective-permute-start.8
  544.8 12.4 %all-to-all-start.2 = ((bf16[32,128,32]{1,2,0:T(8,128)(2,1)}), bf16[32,128,32]{1,2,0:T(8,128)(2,1)S(1)}, u32[]{:S(2)}, u32[]{:S(2)}) async-start(bf16[32,128,32]{1,2,0:T(8,128)(2,1)} %broadcast_in_dim.162), calls=%async_computation.2 | async-start | bytes 524288 | tf_op jit(solution)/shard_map/all_to_all | solution.py:54
  558.0 30.9 %while.36 = (s32[]{:T(128)}, bf16[4,128,128]{2,1,0:T(8,128)(2,1)S(1)}, s32[4]{0:T(128)S(1)}, s32[4,8]{1,0:T(4,128)S(1)}, s32[]{:T(128)}, /*index=5*/s32[4]{0:T(1...) while((s32[]{:T(128)}, ...), condition=%wide.region_31.32_spmd, body=%wide.region_26.31_spmd.sunk | while | flops 69812832 | bytes 5553661 | solution.py:180
  588.9 1.4 convolution_convert_fusion.4
  590.4 3.9 all-to-all-start.3
  594.3 29.2 %all-to-all-done.3 = bf16[8,64,1024]{2,1,0:T(8,128)(2,1)S(1)} async-done(((bf16[8,64,1024]{2,1,0:T(8,128)(2,1)}), bf16[8,64,1024]{2,1,0:T(8,128)(2,1)S(1)}, u32[]{:S(2)}, u32[]{:S(2)}) %all-to-all-start.3) | async-done | bytes 1048608 | tf_op jit(solution)/shard_map/all_to_all | solution.py:77
  623.7 1.6 add_convert_fusion
  (327 shorter events, 84.2 us)
Async XLA Ops:
  7.4 3.2 copy-start.7
  8.9 2.0 copy-start.15
  10.9 74.3 %copy-start.5 = (bf16[512,1024]{1,0:T(8,128)(2,1)}, bf16[512,1024]{1,0:T(8,128)(2,1)S(1)}, u32[]{:S(2)}) copy-start(bf16[512,1024]{1,0:T(8,128)(2,1)S(1)} %fusion.65) | copy-start | bytes 3145732
  84.8 6.6 %copy-start.19 = (bf16[128,32]{0,1:T(8,128)(2,1)S(1)}, bf16[128,32]{0,1:T(8,128)(2,1)}, u32[]{:S(2)}) copy-start(bf16[128,32]{0,1:T(8,128)(2,1)} %param.24) | copy-start | bytes 24580
  84.8 12.3 %copy-start.1 = (bf16[512,1024]{1,0:T(8,128)(2,1)S(1)}, bf16[512,1024]{1,0:T(8,128)(2,1)}, u32[]{:S(2)}) copy-start(bf16[512,1024]{1,0:T(8,128)(2,1)} %param.22) | copy-start | bytes 3145732
  85.7 12.0 %copy-start.22 = (s32[128,8]{0,1:T(8,128)S(1)}, s32[128,8]{0,1:T(8,128)}, u32[]{:S(2)}) copy-start(s32[128,8]{0,1:T(8,128)} %param.31) | copy-start | bytes 12292
  85.7 12.0 %copy-start.23 = (s32[128,8]{0,1:T(8,128)S(1)}, s32[128,8]{0,1:T(8,128)}, u32[]{:S(2)}) copy-start(s32[128,8]{0,1:T(8,128)} %param.33) | copy-start | bytes 12292
  85.7 12.8 %copy-start.24 = (s32[128]{0:T(128)S(1)}, s32[128]{0:T(128)}, u32[]{:S(2)}) copy-start(s32[128]{0:T(128)} %param.32) | copy-start | bytes 1540
  85.8 13.8 %collective-permute-start.1 = (bf16[2,512,128]{2,1,0:T(8,128)(2,1)S(1)}, bf16[2,512,128]{2,1,0:T(8,128)(2,1)S(1)}, u32[]{:S(2)}, u32[]{:S(2)}) collective-permute-start(bf16[2,512,128]{2,1,0:T(8,128)(2,1)S(1)} %pad_maximum_fusion.4), channel_id=1, source_target_pairs={{8,0},{16,8},{24,16},{32,24},{40,32},{48,40},{56,48},{64,56},{72,6... | collective-permute-start | bytes 786440 | tf_op jit(solution)/shard_map/ppermute | solution.py:47
  88.1 11.5 %collective-permute-start = (bf16[2,512,128]{2,1,0:T(8,128)(2,1)S(1)}, bf16[2,512,128]{2,1,0:T(8,128)(2,1)S(1)}, u32[]{:S(2)}, u32[]{:S(2)}) collective-permute-start(bf16[2,512,128]{2,1,0:T(8,128)(2,1)S(1)} %pad_maximum_fusion.4), channel_id=1, source_target_pairs={{0,8},{8,16},{16,24},{24,32},{32,40},{40,48},{48,56},{56,64},{64,7... | collective-permute-start | bytes 786440 | tf_op jit(solution)/shard_map/ppermute | solution.py:44
  92.2 49.8 %all-to-all-start = ((bf16[32,128,32]{1,2,0:T(8,128)(2,1)}), bf16[32,128,32]{1,2,0:T(8,128)(2,1)}, u32[]{:S(2)}, u32[]{:S(2)}) async-start(bf16[32,128,32]{1,2,0:T(8,128)(2,1)} %broadcast_in_dim.157), calls=%async_computation | async-start | bytes 524288 | tf_op jit(solution)/shard_map/all_to_all | solution.py:54
  97.0 165.2 %all-reduce.5.cloned.1.call-start = ((), (), s32[]{:S(2)}) async-start(), calls=%async_computation.4 | async-start | bytes 2097152 | tf_op jit(solution)/shard_map/psum | solution.py:234
  140.8 3.7 copy-start.13
  144.3 26.0 %copy-start.20 = (bf16[128,32]{0,1:T(8,128)(2,1)S(1)}, bf16[128,32]{0,1:T(8,128)(2,1)}, u32[]{:S(2)}) copy-start(bf16[128,32]{0,1:T(8,128)(2,1)} %param.26) | copy-start | bytes 24580
  144.3 43.0 %copy-start.14 = (bf16[32,512]{1,0:T(8,128)(2,1)S(1)}, bf16[32,512]{1,0:T(8,128)(2,1)}, u32[]{:S(2)}) copy-start(bf16[32,512]{1,0:T(8,128)(2,1)} %param.27) | copy-start | bytes 98308
  144.4 205.8 %all-gather.10.cloned.1.call-start = ((), (), s32[]{:S(2)}) async-start(), calls=%async_computation.7 | async-start | bytes 1572864 | tf_op jit(solution)/shard_map/all_gather | solution.py:28
  169.3 55.8 %copy-start.16 = (bf16[3,32,128]{2,1,0:T(8,128)(2,1)S(1)}, bf16[3,32,128]{2,1,0:T(8,128)(2,1)}, u32[]{:S(2)}) copy-start(bf16[3,32,128]{2,1,0:T(8,128)(2,1)} %param.25) | copy-start | bytes 73732
  171.1 177.3 %all-to-all-start.1 = ((bf16[32,128,32]{1,2,0:T(8,128)(2,1)}), bf16[32,128,32]{1,2,0:T(8,128)(2,1)S(1)}, u32[]{:S(2)}, u32[]{:S(2)}) async-start(bf16[32,128,32]{1,2,0:T(8,128)(2,1)} %broadcast_in_dim.159), calls=%async_computation.1 | async-start | bytes 524288 | tf_op jit(solution)/shard_map/all_to_all | solution.py:54
  187.3 165.7 %all-gather.8.cloned.1.call-start = ((), (), s32[]{:S(2)}) async-start(), calls=%async_computation.6 | async-start | bytes 1572864 | tf_op jit(solution)/shard_map/all_gather | solution.py:28
  225.0 207.4 %all-reduce.7.cloned.1.call-start = ((), (), s32[]{:S(2)}) async-start(), calls=%async_computation.5 | async-start | bytes 2097152 | tf_op jit(solution)/shard_map/psum | solution.py:276
  262.2 1.7 copy-start.4
  264.8 5.0 copy-start.9
  265.8 13.7 %collective-permute-start.2 = (bf16[2,512,128]{2,1,0:T(8,128)(2,1)S(1)}, bf16[2,512,128]{2,1,0:T(8,128)(2,1)}, u32[]{:S(2)}, u32[]{:S(2)}) collective-permute-start(bf16[2,512,128]{2,1,0:T(8,128)(2,1)S(1)} %pad_maximum_fusion.5), channel_id=1, source_target_pairs={{0,24},{8,32},{16,40},{24,48},{32,56},{40,64},{48,72},{56,80},{64,... | collective-permute-start | bytes 786440 | tf_op jit(solution)/shard_map/ppermute | solution.py:66
  269.9 11.8 %collective-permute-start.3 = (bf16[2,512,128]{2,1,0:T(8,128)(2,1)S(1)}, bf16[2,512,128]{2,1,0:T(8,128)(2,1)S(1)}, u32[]{:S(2)}, u32[]{:S(2)}) collective-permute-start(bf16[2,512,128]{2,1,0:T(8,128)(2,1)S(1)} %pad_maximum_fusion.5), channel_id=1, source_target_pairs={{0,16},{8,24},{16,32},{24,40},{32,48},{40,56},{48,64},{56,72},{64,... | collective-permute-start | bytes 786440 | tf_op jit(solution)/shard_map/ppermute | solution.py:66
  273.2 10.5 %collective-permute-start.4 = (bf16[2,512,128]{2,1,0:T(8,128)(2,1)S(1)}, bf16[2,512,128]{2,1,0:T(8,128)(2,1)S(1)}, u32[]{:S(2)}, u32[]{:S(2)}) collective-permute-start(bf16[2,512,128]{2,1,0:T(8,128)(2,1)S(1)} %pad_maximum_fusion.5), channel_id=1, source_target_pairs={{0,8},{8,16},{16,24},{24,32},{32,40},{40,48},{48,56},{56,64},{64,7... | collective-permute-start | bytes 786440 | tf_op jit(solution)/shard_map/ppermute | solution.py:66
  275.7 9.1 %collective-permute-start.5 = (bf16[2,512,128]{2,1,0:T(8,128)(2,1)S(1)}, bf16[2,512,128]{2,1,0:T(8,128)(2,1)S(1)}, u32[]{:S(2)}, u32[]{:S(2)}) collective-permute-start(bf16[2,512,128]{2,1,0:T(8,128)(2,1)S(1)} %pad_maximum_fusion.5), channel_id=1, source_target_pairs={{8,0},{16,8},{24,16},{32,24},{40,32},{48,40},{56,48},{64,56},{72,6... | collective-permute-start | bytes 786440 | tf_op jit(solution)/shard_map/ppermute | solution.py:66
  277.7 10.2 %collective-permute-start.6 = (bf16[2,512,128]{2,1,0:T(8,128)(2,1)S(1)}, bf16[2,512,128]{2,1,0:T(8,128)(2,1)S(1)}, u32[]{:S(2)}, u32[]{:S(2)}) collective-permute-start(bf16[2,512,128]{2,1,0:T(8,128)(2,1)S(1)} %pad_maximum_fusion.5), channel_id=1, source_target_pairs={{16,0},{24,8},{32,16},{40,24},{48,32},{56,40},{64,48},{72,56},{80,... | collective-permute-start | bytes 786440 | tf_op jit(solution)/shard_map/ppermute | solution.py:66
  279.4 18.6 %collective-permute-start.7 = (bf16[2,512,128]{2,1,0:T(8,128)(2,1)S(1)}, bf16[2,512,128]{2,1,0:T(8,128)(2,1)S(1)}, u32[]{:S(2)}, u32[]{:S(2)}) collective-permute-start(bf16[2,512,128]{2,1,0:T(8,128)(2,1)S(1)} %pad_maximum_fusion.5), channel_id=1, source_target_pairs={{24,0},{32,8},{40,16},{48,24},{56,32},{64,40},{72,48},{80,56},{88,... | collective-permute-start | bytes 786440 | tf_op jit(solution)/shard_map/ppermute | solution.py:66
  298.1 1.3 copy-start
  306.3 2.0 copy-start.3
  308.8 1.1 copy-start.2
  318.6 2.0 copy-start.3
  321.0 1.1 copy-start.2
  330.8 2.0 copy-start.3
  333.3 1.1 copy-start.2
  343.1 2.0 copy-start.3
  345.6 1.1 copy-start.2
  349.9 179.4 %all-reduce.9.cloned.1.call-start = ((), (), s32[]{:S(2)}) async-start(), calls=%async_computation.8 | async-start | bytes 2097152 | tf_op jit(solution)/shard_map/psum | solution.py:285
  434.5 1.2 copy-start.10
  435.7 5.7 copy-start.17
  529.3 1.6 copy-start.8
  531.4 1.0 copy-start.12
  531.4 1.4 copy-start.11
  531.7 12.3 %copy-start.21 = (bf16[128,32]{0,1:T(8,128)(2,1)S(1)}, bf16[128,32]{0,1:T(8,128)(2,1)}, u32[]{:S(2)}) copy-start(bf16[128,32]{0,1:T(8,128)(2,1)} %param.30) | copy-start | bytes 24580
  532.3 24.9 %copy-start.18 = (s32[4,8]{0,1:T(8,128)S(1)}, s32[4,8]{0,1:T(8,128)}, u32[]{:S(2)}) copy-start(s32[4,8]{0,1:T(8,128)} %get-tuple-element.308) | copy-start | bytes 388
  532.3 25.0 %copy-start.25 = (s32[128]{0:T(128)S(1)}, s32[128]{0:T(128)}, u32[]{:S(2)}) copy-start(s32[128]{0:T(128)} %param.34) | copy-start | bytes 1540
  532.3 25.1 %copy-start.6 = (bf16[512,1024]{1,0:T(8,128)(2,1)S(1)}, bf16[512,1024]{1,0:T(8,128)(2,1)}, u32[]{:S(2)}) copy-start(bf16[512,1024]{1,0:T(8,128)(2,1)} %copy-done.5) | copy-start | bytes 3145732
  533.3 24.6 %collective-permute-start.9 = (bf16[2,512,128]{2,1,0:T(8,128)(2,1)S(1)}, bf16[2,512,128]{2,1,0:T(8,128)(2,1)S(1)}, u32[]{:S(2)}, u32[]{:S(2)}) collective-permute-start(bf16[2,512,128]{2,1,0:T(8,128)(2,1)S(1)} %pad_maximum_fusion.6), channel_id=1, source_target_pairs={{8,0},{16,8},{24,16},{32,24},{40,32},{48,40},{56,48},{64,56},{72,6... | collective-permute-start | bytes 786440 | tf_op jit(solution)/shard_map/ppermute | solution.py:47
  540.9 17.0 %collective-permute-start.8 = (bf16[2,512,128]{2,1,0:T(8,128)(2,1)S(1)}, bf16[2,512,128]{2,1,0:T(8,128)(2,1)S(1)}, u32[]{:S(2)}, u32[]{:S(2)}) collective-permute-start(bf16[2,512,128]{2,1,0:T(8,128)(2,1)S(1)} %pad_maximum_fusion.6), channel_id=1, source_target_pairs={{0,8},{8,16},{16,24},{24,32},{32,40},{40,48},{48,56},{56,64},{64,7... | collective-permute-start | bytes 786440 | tf_op jit(solution)/shard_map/ppermute | solution.py:44
  544.8 44.1 %all-to-all-start.2 = ((bf16[32,128,32]{1,2,0:T(8,128)(2,1)}), bf16[32,128,32]{1,2,0:T(8,128)(2,1)S(1)}, u32[]{:S(2)}, u32[]{:S(2)}) async-start(bf16[32,128,32]{1,2,0:T(8,128)(2,1)} %broadcast_in_dim.162), calls=%async_computation.2 | async-start | bytes 524288 | tf_op jit(solution)/shard_map/all_to_all | solution.py:54
  590.4 33.1 %all-to-all-start.3 = ((bf16[8,64,1024]{2,1,0:T(8,128)(2,1)}), bf16[8,64,1024]{2,1,0:T(8,128)(2,1)S(1)}, u32[]{:S(2)}, u32[]{:S(2)}) async-start(bf16[8,64,1024]{2,1,0:T(8,128)(2,1)} %bitcast.85), calls=%async_computation.3 | async-start | bytes 2097152 | tf_op jit(solution)/shard_map/all_to_all | solution.py:77
Sparse Core Ops, SparseCore 0:
  144.5 84.8 all-reduce.4
  350.0 82.4 all-reduce.6
  441.5 87.7 all-reduce.8
Sparse Core Ops, SparseCore 1:
  170.4 29.2 all-gather.9
  225.1 29.3 all-gather.7
where the time goes:
time: 635 us; the launch traced here: 632 us
  blocking collectives  214 us (34%)
  waiting for transfers between devices  169 us (27%)
  starting transfers between devices  68.7 us (11%)
  local copies, waits for them, and re-layouts  64.8 us (10%)
  matrix products  41.6 us (7%)
  other arithmetic  33 us (5%)
  loops' own time  26.2 us (4%)
  between operations  15.4 us (2%)
    all_gather x8, blocking collectives, all_blocks(): blocks = lax.all_gather(blocks, axes[k], axis=0, tiled=True)  214 us
    psum x1, waiting for transfers between devices, per_device(): lax.psum(proc_terms.astype(jnp.bfloat16), 'head').astype(jnp.float32)  77.1 us
    psum x1, waiting for transfers between devices, per_device(): lax.psum(ff_terms.astype(jnp.bfloat16), 'head').astype(jnp.float32)  45.9 us
    all_to_all x3, starting transfers between devices, copy_for_each(): lax.all_to_all(jnp.broadcast_to(array[None], (size, *array.shape)), axis,...  33.5 us
    all_to_all x1, waiting for transfers between devices, summed_on_arrival(): blocks = lax.all_to_all(split_up(array, dim, size), axis, 0, 0, tiled=True)  29.2 us
    another operation x2, loops' own time, listed_attend(): result = lax.map(one_block, jnp.arange(rows // BLOCK, dtype=jnp.int32))  20.8 us
    ppermute x6, waiting for transfers between devices, shifted(): return lax.ppermute(block, axis, route)  16.1 us
    dot_general x24, matrix products, head_scores(): jnp.einsum('qd,kd->qk', queries[:, lower:lower + HD], key_rows[:, lower:l...  15 us
  transfers between devices with their start and end apart: 19, of which 7 were waited for; matrix products, arithmetic and copies ran while one was open for 18% of the time, Pallas kernels for 0%

commit v1 on v0

v1 whole, which is shorter than its diff:
```python
import functools

import jax
import jax.numpy as jnp
from jax import lax
from jax.experimental import pallas as pl
from jax.experimental.pallas import tpu as pltpu
from jax.sharding import PartitionSpec as P

HD = 64
BLOCK = 128
WINDOW = 1536
REACH = 3
EPSILON = 1e-05
NEGATIVE = -1e30
SCALE = HD ** (-0.5) * 1.4426950408889634
MESH_ID = pl.DeviceIdType.MESH


def contract_rows(left, right):
    return lax.dot_general(left, right, (((1,), (1,)), ((), ())), preferred_element_type=jnp.float32)


def normed(values):
    centred = values - jnp.mean(values, axis=-1, keepdims=True)
    variance = jnp.mean(centred * centred, axis=-1, keepdims=True)
    return (centred * lax.rsqrt(variance + EPSILON)).astype(jnp.bfloat16)


def kernel(
    nb,
    nh,
    grid_ref,
    mesh_ref,
    w_ref,
    enc_bias,
    dec_bias,
    key_ids,
    query_ids,
    out_ref,
    wall,
    x,
    gn,
    q,
    attn,
    hidden,
    p,
    slots,
    eslab,
    wslab,
    dslab,
    state,
    zs,
    zr,
    ps,
    pr,
    rss,
    rsr,
    ags,
    agr,
    hs,
    hr,
):
    b = lax.axis_index("band")
    h = lax.axis_index("head")
    rows, depth = grid_ref.shape
    width = q.shape[1]
    ff = hidden.shape[1]
    share = rows // nh
    half_cols = depth // 2
    wrows = w_ref.shape[0]
    nz = nb // 2
    odd = lax.rem(b, 2)
    partner = b + 1 - 2 * odd
    stages = (
        (0, 4 * width),
        (4 * width, 8 * width),
        (8 * width, 8 * width + 2 * ff),
        (8 * width + 2 * ff, 12 * width + 2 * ff),
    )

    def band(offset):
        return lax.rem(b + (offset + nb), nb)

    def head(offset):
        return lax.rem(h + (offset + nh), nh)

    def copy(src, dst, send_sem, recv_sem, **where):
        return pltpu.make_async_remote_copy(
            src_ref=src,
            dst_ref=dst,
            send_sem=send_sem,
            recv_sem=recv_sem,
            device_id={"band": where.get("band", b), "head": where.get("head", h)},
            device_id_type=MESH_ID,
        )

    sent = []

    barrier = pltpu.get_barrier_semaphore()
    peers = [{"band": band(o), "head": h} for o in (1, -1, 2, -2, 3, -3)]
    peers += [{"band": b, "head": head(o)} for o in (1, -1)]
    for peer in peers:
        pl.semaphore_signal(barrier, inc=1, device_id=peer, device_id_type=MESH_ID)
    pl.semaphore_wait(barrier, len(peers))

    right_steps = nz // 2
    left_steps = nz - 1 - right_steps

    def block(index, stage):
        low, high = stages[stage]
        return wall.at[pl.ds(pl.multiple_of(index * wrows, wrows), wrows), low:high]

    def own(stage):
        low, high = stages[stage]
        return w_ref.at[:, low:high]

    def zcopy(stage, way, step):
        index = band(2 * step if way else -2 * step)
        src = block(index, stage) if step else own(stage)
        return copy(
            src,
            block(index, stage),
            zs.at[stage, way, step],
            zr.at[stage, way, step],
            band=band(-2 if way else 2),
        )

    def pcopy(stage, k):
        index = band(2 * k)
        src = block(index, stage) if k else own(stage)
        return copy(src, block(index, stage), ps.at[stage, k], pr.at[stage, k], band=partner)

    def begin(one):
        one.start()
        sent.append(one)

    def zstart(stage):
        begin(zcopy(stage, 0, 0))
        if left_steps:
            begin(zcopy(stage, 1, 0))
        begin(pcopy(stage, 0))
        low, high = stages[stage]
        wall[pl.ds(pl.multiple_of(b * wrows, wrows), wrows), low:high] = w_ref[:, low:high]

    def zstep(stage, step):
        if step > right_steps:
            return
        zcopy(stage, 0, step - 1).wait_recv()
        if step < right_steps:
            begin(zcopy(stage, 0, step))
        begin(pcopy(stage, nz - step))
        if step - 1 < left_steps:
            zcopy(stage, 1, step - 1).wait_recv()
            if step < left_steps:
                begin(zcopy(stage, 1, step))
            begin(pcopy(stage, step))

    def zfinish(stage):
        for k in range(nz):
            pcopy(stage, k).wait_recv()

    longer = nh // 2
    shorter = nh - 1 - longer
    flows = ((1, 0, longer), (-1, 1, longer), (1, 1, shorter), (-1, 0, shorter))
    base = (0, longer, 2 * longer, 2 * longer + shorter)

    def share_rows(chunk):
        return pl.ds(pl.multiple_of(chunk * share, share), share)

    def half_of(half):
        return slice(half * half_cols, (half + 1) * half_cols)

    def rcopy(stage, flow, step):
        way, half, hops = flows[flow]
        slot = base[flow] + step
        return copy(
            p.at[share_rows(head(way * (hops - step))), half_of(half)],
            slots.at[slot],
            rss.at[stage, slot],
            rsr.at[stage, slot],
            head=head(way),
        )

    def acopy(stage, flow, step):
        way, half, hops = flows[flow]
        slot = base[flow] + step
        view = x.at[share_rows(head(-way * step)), half_of(half)]
        return copy(view, view, ags.at[stage, slot], agr.at[stage, slot], head=head(way))

    def summed(stage, next_stage):
        for step in range(longer):
            for flow, (way, half, hops) in enumerate(flows):
                if step < hops:
                    if step:
                        rcopy(stage, flow, step - 1).wait_recv()
                        where = share_rows(head(way * (hops - step)))
                        p[where, half_of(half)] = (
                            p[where, half_of(half)].astype(jnp.float32)
                            + slots[base[flow] + step - 1].astype(jnp.float32)
                        ).astype(jnp.bfloat16)
                    rcopy(stage, flow, step).start()
            if next_stage is not None:
                zstep(next_stage, step + 1)
        halves = [p[share_rows(h), half_of(half)].astype(jnp.float32) for half in range(2)]
        for flow, (way, half, hops) in enumerate(flows):
            rcopy(stage, flow, hops - 1).wait_recv()
            halves[half] = halves[half] + slots[base[flow] + hops - 1].astype(jnp.float32)
        for flow, (way, half, hops) in enumerate(flows):
            for step in range(hops):
                rcopy(stage, flow, step).wait_send()
        return jnp.concatenate(halves, axis=1)

    def gathered(stage, next_stage):
        for step in range(longer):
            for flow, (way, half, hops) in enumerate(flows):
                if step < hops:
                    if step:
                        acopy(stage, flow, step - 1).wait_recv()
                    acopy(stage, flow, step).start()
            zstep(next_stage, longer + step + 1)
        for flow, (way, half, hops) in enumerate(flows):
            acopy(stage, flow, hops - 1).wait_recv()
        for flow, (way, half, hops) in enumerate(flows):
            for step in range(hops):
                acopy(stage, flow, step).wait_send()
        for step in range(2 * longer + 1, right_steps + 1):
            zstep(next_stage, step)
        zfinish(next_stage)

    tile = min(256, rows)
    tiles = rows // tile

    def tile_rows(index, offset=0):
        return pl.ds(pl.multiple_of(offset + index * tile, tile), tile)

    def for_tiles(body):
        @pl.loop(0, tiles)
        def _(index):
            body(index)

    def norm_rows(src, dst):
        piece = min(64, rows)

        @pl.loop(0, rows // piece)
        def _(index):
            where = pl.ds(pl.multiple_of(index * piece, piece), piece)
            dst[where, :] = normed(src[where, :].astype(jnp.float32))

    def project_q(stage, src):
        low = stages[stage][0]

        def body(index):
            q[tile_rows(index), :] = jnp.dot(
                src[tile_rows(index), :], wall[:, low : low + width], preferred_element_type=jnp.float32
            ).astype(jnp.bfloat16)

        for_tiles(body)

    def project_kv(stage, src, slab, offset):
        low = stages[stage][0]

        def body(index):
            slab[tile_rows(index, offset), :] = jnp.dot(
                src[tile_rows(index), :],
                wall[:, low + width : low + 3 * width],
                preferred_element_type=jnp.float32,
            ).astype(jnp.bfloat16)

        for_tiles(body)

    def project_out(stage):
        low = stages[stage][0] + 3 * width

        def body(index):
            p[tile_rows(index), :] = contract_rows(
                attn[tile_rows(index), :], wall[:, low : low + width]
            ).astype(jnp.bfloat16)

        for_tiles(body)

    def attend(slab, mask, keys, moving):
        lane = lax.broadcasted_iota(jnp.int32, (BLOCK, width), 1)

        @pl.loop(0, rows // BLOCK)
        def _(index):
            where = pl.ds(pl.multiple_of(index * BLOCK, BLOCK), BLOCK)
            taken = pl.ds(pl.multiple_of(index * BLOCK, BLOCK), keys) if moving else pl.ds(0, keys)
            query = q[where, :]
            zero = jnp.zeros_like(query)
            both = jnp.concatenate(
                [jnp.where(lane < HD, query, zero), jnp.where(lane < HD, zero, query)], axis=0
            )
            scores = mask(contract_rows(both, slab[taken, 0:width]), index, where, taken)
            maxima = jnp.max(scores, axis=1, keepdims=True)
            expo = jnp.exp2((scores - maxima) * SCALE)
            totals = jnp.sum(expo, axis=1, keepdims=True)
            mixed = jnp.dot(
                expo.astype(jnp.bfloat16),
                slab[taken, width : 2 * width],
                preferred_element_type=jnp.float32,
            )
            mixed = mixed / totals
            attn[where, :] = jnp.where(lane < HD, mixed[:BLOCK], mixed[BLOCK:]).astype(jnp.bfloat16)

    def listed_mask(bias):
        def mask(scores, index, where, taken):
            return scores + bias[pl.ds(index, 1), :]

        return mask

    def window_mask(scores, index, where, taken):
        ids = query_ids[where, :]
        same = jnp.concatenate([ids, ids], axis=0) == key_ids[:, taken]
        return jnp.where(same, scores, NEGATIVE)

    def swap_sides(slab, first):
        view = slab.at[pl.ds(rows, rows), :]
        moves = [
            copy(
                view,
                slab.at[pl.ds((1 - o) * rows, rows), :],
                hs.at[first + k],
                hr.at[first + k],
                band=band(o),
            )
            for k, o in enumerate((1, -1))
        ]
        for move in moves:
            begin(move)
        return moves

    zstart(0)
    norm_rows(mesh_ref, x)
    zstep(0, 1)
    norm_rows(grid_ref, gn)
    for step in range(2, right_steps + 1):
        zstep(0, step)
    zfinish(0)
    zstart(1)
    project_kv(0, gn, eslab, rows)
    moves = swap_sides(eslab, 0)
    project_q(0, x)
    for move in moves:
        move.wait_recv()
    attend(eslab, listed_mask(enc_bias), 3 * rows, False)
    project_out(0)
    mine = share_rows(h)
    state[...] = mesh_ref[mine, :].astype(jnp.float32) + summed(0, 1)
    x[mine, :] = normed(state[...])
    gathered(0, 1)

    zstart(2)
    project_kv(1, x, wslab, REACH * rows)
    view = wslab.at[pl.ds(REACH * rows, rows), :]

    def part(place):
        return wslab.at[pl.ds(pl.multiple_of(place * rows, rows), rows), :]

    moves = [
        copy(view, part(1), hs.at[2], hr.at[2], band=band(2)),
        copy(view, part(5), hs.at[3], hr.at[3], band=band(-2)),
        copy(view, part(2 + 2 * odd), hs.at[4], hr.at[4], band=partner),
        copy(view, part(6 - 6 * odd), hs.at[5], hr.at[5], band=lax.rem(b + 6 * odd - 3 + nb, nb)),
    ]
    for move in moves:
        begin(move)
    project_q(1, x)
    passed = [
        copy(part(1), part(2 * odd), hs.at[6], hr.at[6], band=partner),
        copy(part(5), part(4 + 2 * odd), hs.at[7], hr.at[7], band=partner),
    ]
    for move, onward in zip(moves, passed):
        move.wait_recv()
        begin(onward)
    for move in (moves[2], moves[3], *passed):
        move.wait_recv()
    attend(wslab, window_mask, 2 * REACH * rows + BLOCK, True)
    project_out(1)
    state[...] = state[...] + summed(1, 2)
    x[mine, :] = normed(state[...])
    gathered(1, 2)

    zstart(3)
    low = stages[2][0]

    def feed(index):
        inner = jnp.dot(
            x[tile_rows(index), :], wall[:, low : low + ff], preferred_element_type=jnp.float32
        )
        hidden[tile_rows(index), :] = (inner * 0.5 * (1.0 + lax.erf(inner * 0.5**0.5))).astype(
            jnp.bfloat16
        )
        p[tile_rows(index), :] = contract_rows(
            hidden[tile_rows(index), :], wall[:, low + ff : low + 2 * ff]
        ).astype(jnp.bfloat16)

    for_tiles(feed)
    state[...] = state[...] + summed(2, 3)
    x[mine, :] = normed(state[...])
    gathered(2, 3)

    project_kv(3, x, dslab, rows)
    moves = swap_sides(dslab, 8)
    project_q(3, gn)
    for move in moves:
        move.wait_recv()
    attend(dslab, listed_mask(dec_bias), 3 * rows, False)
    project_out(3)
    out_ref[...] = (grid_ref[mine, :].astype(jnp.float32) + summed(3, None)).astype(jnp.bfloat16)
    for move in sent:
        move.wait_send()


def listed_bias(lists, counts, b, blocks, keys_per_block):
    my_lists = lax.dynamic_slice_in_dim(lists, b * blocks, blocks, 0) - (b - 1) * keys_per_block
    my_counts = lax.dynamic_slice_in_dim(counts, b * blocks, blocks, 0)
    live = jnp.arange(lists.shape[1], dtype=jnp.int32)[None, :] < my_counts[:, None]
    places = jnp.arange(3 * keys_per_block * BLOCK, dtype=jnp.int32) // BLOCK
    hit = (my_lists[:, :, None] == places[None, None, :]) & live[:, :, None]
    return jnp.where(jnp.any(hit, axis=1), 0.0, NEGATIVE).astype(jnp.float32)


def per_device(
    nb,
    nh,
    grid_feats,
    mesh_feats,
    enc_in,
    enc_out,
    proc_in,
    proc_out,
    ff_up,
    ff_down,
    dec_in,
    dec_out,
    enc_list,
    enc_count,
    dec_list,
    dec_count,
    window_ids,
):
    b = lax.axis_index("band")
    rows, depth = mesh_feats.shape
    assert grid_feats.shape == mesh_feats.shape and WINDOW <= REACH * rows
    width = enc_in.shape[2]
    ff = ff_up.shape[1]
    share = rows // nh
    nz = nb // 2
    w = jnp.concatenate(
        [
            *(enc_in[k] for k in range(3)),
            enc_out.T,
            *(proc_in[k] for k in range(3)),
            proc_out.T,
            ff_up,
            ff_down.T,
            *(dec_in[k] for k in range(3)),
            dec_out.T,
        ],
        axis=1,
    )
    blocks = rows // BLOCK
    enc_bias = listed_bias(enc_list, enc_count, b, blocks, blocks)
    dec_bias = listed_bias(dec_list, dec_count, b, blocks, blocks)
    padded = jnp.pad(window_ids, (REACH * rows, REACH * rows), constant_values=-1)
    key_ids = lax.dynamic_slice_in_dim(padded, b * rows, (2 * REACH + 1) * rows, 0)[None, :]
    query_ids = lax.dynamic_slice_in_dim(window_ids, b * rows, rows, 0)[:, None]
    bf16, f32 = jnp.bfloat16, jnp.float32
    dma = pltpu.SemaphoreType.DMA
    msgs = 2 * (nh - 1)
    vmem = pl.BlockSpec(memory_space=pltpu.VMEM)
    return pl.pallas_call(
        functools.partial(kernel, nb, nh),
        out_shape=jax.ShapeDtypeStruct((share, depth), bf16),
        in_specs=[vmem] * 7,
        out_specs=vmem,
        scratch_shapes=[
            pltpu.VMEM((nb * w.shape[0], w.shape[1]), bf16),
            pltpu.VMEM((rows, depth), bf16),
            pltpu.VMEM((rows, depth), bf16),
            pltpu.VMEM((rows, width), bf16),
            pltpu.VMEM((rows, width), bf16),
            pltpu.VMEM((rows, ff), bf16),
            pltpu.VMEM((rows, depth), bf16),
            pltpu.VMEM((msgs, share, depth // 2), bf16),
            pltpu.VMEM((3 * rows, 2 * width), bf16),
            pltpu.VMEM(((2 * REACH + 1) * rows, 2 * width), bf16),
            pltpu.VMEM((3 * rows, 2 * width), bf16),
            pltpu.VMEM((share, depth), f32),
            dma((4, 2, nz // 2)),
            dma((4, 2, nz // 2)),
            dma((4, nz)),
            dma((4, nz)),
            dma((4, msgs)),
            dma((4, msgs)),
            dma((3, msgs)),
            dma((3, msgs)),
            dma((10,)),
            dma((10,)),
        ],
        compiler_params=pltpu.CompilerParams(
            collective_id=0, has_side_effects=True, vmem_limit_bytes=60 * 1024 * 1024
        ),
    )(grid_feats, mesh_feats, w, enc_bias, dec_bias, key_ids, query_ids)


def solution(mesh):
    rows = P(("members", "band"), None)
    placed = (
        rows,
        rows,
        P(None, "band", "head"),
        P("head", "band"),
        P(None, "band", "head"),
        P("head", "band"),
        P("band", "head"),
        P("head", "band"),
        P(None, "band", "head"),
        P("head", "band"),
        P(),
        P(),
        P(),
        P(),
        P(),
    )
    return jax.shard_map(
        functools.partial(per_device, mesh.shape["band"], mesh.shape["head"]),
        mesh=mesh,
        in_specs=placed,
        out_specs=P(("members", "band", "head"), None),
        check_vma=False,
    )
```

time: 635 us -> 238 us (0.37)
  Pallas kernels: 0 us -> 225 us
  blocking collectives: 214 us -> 0 us
  waiting for transfers between devices: 169 us -> 0 us
  starting transfers between devices: 68.7 us -> 0 us
  local copies, waits for them, and re-layouts: 64.8 us -> 9.23 us
  matrix products: 41.6 us -> 0 us
  other arithmetic: 33 us -> 2.32 us
  loops' own time: 26.2 us -> 0 us
  between operations: 15.4 us -> 0.06 us
    pallas_call x0 -> x1, Pallas kernels: none -> 225 us  [per_device(): pl.pallas_call(functools.partial(kernel, nb, nh), out_shape=jax.ShapeDtyp...]
    all_gather x8 -> x0, blocking collectives: 214 us -> none  [all_blocks(): blocks = lax.all_gather(blocks, axes[k], axis=0, tiled=True)]
    psum x3 -> x0, waiting for transfers between devices: 123 us -> none  [the longest x1 77.1 us: per_device(): lax.psum(proc_terms.astype(jnp.bfloat16), 'head').astype(jnp.float32)]
    dot_general x61 -> x0, matrix products: 41.6 us -> none  [the longest x24 15 us: head_scores(): jnp.einsum('qd,kd->qk', queries[:, lower:lower + HD], key_rows[:, lower:l...]
    all_to_all x4 -> x0, starting transfers between devices: 37.4 us -> none  [the longest x3 33.5 us: copy_for_each(): lax.all_to_all(jnp.broadcast_to(array[None], (size, *array.shape)), axis,...]
    ppermute x10 -> x0, starting transfers between devices: 30.8 us -> none  [the longest x6 14.4 us: shifted(): return lax.ppermute(block, axis, route)]
    all_to_all x4 -> x0, waiting for transfers between devices: 29.2 us -> none  [the longest x1 29.2 us: summed_on_arrival(): blocks = lax.all_to_all(split_up(array, dim, size), axis, 0, 0, tiled=True)]
    another operation x3 -> x0, loops' own time: 26.2 us -> none  [the longest x2 20.8 us: listed_attend(): result = lax.map(one_block, jnp.arange(rows // BLOCK, dtype=jnp.int32))]
  transfers between devices with their start and end apart: 19 -> 0, of which waited for: 7 -> 0; matrix products, arithmetic and copies ran while one was open for 18% -> 0% of each run, Pallas kernels for 0% -> 0%
where the time goes in v1:
time: 238 us; the launch traced here: 237 us
  Pallas kernels  225 us (95%)
  local copies, waits for them, and re-layouts  9.23 us (4%)
    pallas_call x1, Pallas kernels, per_device(): pl.pallas_call(functools.partial(kernel, nb, nh), out_shape=jax.ShapeDtyp...  225 us
    unnamed x34, local copies, waits for them, and re-layouts  5.26 us

profile of v1, /device:TPU:65, one launch (start us, length us, event | category | flops | bytes accessed | tf_op | source)
XLA Modules:
  0.0 236.8 jit_solution(13507084620930725070)
XLA Ops:
  0.0 0.0 copy-start.1
  0.0 0.8 dynamic_slice.19
  0.8 0.7 dynamic_slice.21
  1.5 0.1 iota_compare_fusion
  1.6 0.8 dynamic_slice.23
  2.3 0.8 dynamic-slice_subtract_fusion
  3.1 0.1 copy.22
  3.2 0.1 copy.21
  3.3 0.2 and_reduce_fusion
  3.5 0.0 copy-done.1
  3.5 0.1 pad_dynamic-slice_fusion
  3.6 0.6 broadcast_in_dim.28.key_ids
  4.2 0.0 copy-start.4
  4.2 0.6 broadcast_select_fusion.dec_bias
  4.8 0.6 broadcast_select_fusion.1.enc_bias
  5.5 0.0 copy-done.4
  5.5 0.0 copy-start.5
  5.5 0.0 copy-start.7
  5.5 0.7 copy-done.7
  6.2 0.0 copy-done.5
  6.2 0.0 copy-start.2
  6.2 0.0 copy-start.8
  6.2 0.7 copy-done.8
  6.9 0.0 copy-done.2
  7.0 0.0 copy-start.3
  7.0 0.8 copy-done.3
  7.7 0.0 copy-start.6
  7.7 0.7 copy-done.6
  8.5 0.0 copy-start.9
  8.5 0.7 copy-done.9
  9.2 0.0 copy-start
  9.2 0.9 copy.23.query_ids
  10.0 0.0 copy-done
  10.0 225.2 %shard_map.145 = bf16[64,1024]{1,0:T(8,128)(2,1)} custom-call(bf16[512,1024]{1,0:T(8,128)(2,1)} %grid_ref.1, bf16[512,1024]{1,0:T(8,128)(2,1)} %mesh_ref.1, bf16[32,2560]{1,0:T(8,128)(2,1)} %copy-done, f32[4,1536]{1,0:T(4,128)} %broadcast_select_fusion.1.enc_bias, f32[4,1536]{1,0:T(4,128)} %broadcast_select_fusion.dec_bias, ...), custom_call_target="tpu_custom_call" | custom-call | tf_op jit(solution)/shard_map/pallas_call | solution.py:473
  235.2 1.6 copy.38
  (15 shorter events, 0.1 us)
Async XLA Ops:
  0.0 3.5 %copy-start.1 = (s32[16384]{0:T(1024)S(1)}, s32[16384]{0:T(1024)}, u32[]{:S(2)}) copy-start(s32[16384]{0:T(1024)} %param.29) | copy-start | bytes 196612
  4.2 1.2 copy-start.4
  5.5 0.7 copy-start.5
  5.5 0.7 copy-start.7
  6.2 0.8 copy-start.2
  6.2 0.7 copy-start.8
  7.0 0.8 copy-start.3
  7.7 0.7 copy-start.6
  8.5 0.7 copy-start.9
  9.2 0.9 copy-start

commit v2 on v1

v2 whole, which is shorter than its diff:
```python
import functools

import jax
import jax.numpy as jnp
from jax import lax
from jax.experimental import pallas as pl
from jax.experimental.pallas import tpu as pltpu
from jax.sharding import PartitionSpec as P

HD = 64
BLOCK = 128
WINDOW = 1536
REACH = 3
GROUPS = 2
EPSILON = 1e-05
NEGATIVE = -1e30
SCALE = HD ** (-0.5) * 1.4426950408889634
MESH_ID = pl.DeviceIdType.MESH


def contract_rows(left, right):
    return lax.dot_general(left, right, (((1,), (1,)), ((), ())), preferred_element_type=jnp.float32)


def normed(values):
    centred = values - jnp.mean(values, axis=-1, keepdims=True)
    variance = jnp.mean(centred * centred, axis=-1, keepdims=True)
    return (centred * lax.rsqrt(variance + EPSILON)).astype(jnp.bfloat16)


def kernel(
    nb,
    nh,
    grid_ref,
    mesh_ref,
    w_ref,
    enc_bias,
    dec_bias,
    key_ids,
    query_ids,
    out_ref,
    wall,
    x,
    gn,
    q,
    p,
    slots,
    eslab,
    wslab,
    dslab,
    state,
    zs,
    zr,
    ps,
    pr,
    rss,
    rsr,
    ags,
    agr,
    hs,
    hr,
):
    b = lax.axis_index("band")
    h = lax.axis_index("head")
    rows, depth = grid_ref.shape
    width = q.shape[1]
    ff = (w_ref.shape[1] - 12 * width) // 2
    share = rows // nh
    half_cols = depth // 2
    wrows = w_ref.shape[0]
    nz = nb // 2
    odd = lax.rem(b, 2)
    partner = b + 1 - 2 * odd
    stages = (
        (0, 4 * width),
        (4 * width, 8 * width),
        (8 * width, 8 * width + 2 * ff),
        (8 * width + 2 * ff, 12 * width + 2 * ff),
    )

    def band(offset):
        return lax.rem(b + (offset + nb), nb)

    def head(offset):
        return lax.rem(h + (offset + nh), nh)

    def copy(src, dst, send_sem, recv_sem, **where):
        return pltpu.make_async_remote_copy(
            src_ref=src,
            dst_ref=dst,
            send_sem=send_sem,
            recv_sem=recv_sem,
            device_id={"band": where.get("band", b), "head": where.get("head", h)},
            device_id_type=MESH_ID,
        )

    barrier = pltpu.get_barrier_semaphore()
    peers = [{"band": band(o), "head": h} for o in (1, -1, 2, -2, 3, -3)]
    peers += [{"band": b, "head": head(o)} for o in (1, -1)]
    for peer in peers:
        pl.semaphore_signal(barrier, inc=1, device_id=peer, device_id_type=MESH_ID)
    pl.semaphore_wait(barrier, len(peers))

    right_steps = nz // 2
    left_steps = nz - 1 - right_steps

    def block(index, stage):
        low, high = stages[stage]
        return wall.at[pl.ds(pl.multiple_of(index * wrows, wrows), wrows), low:high]

    def own(stage):
        low, high = stages[stage]
        return w_ref.at[:, low:high]

    def zcopy(stage, way, step, first=False):
        index = band(2 * step if way else -2 * step)
        return copy(
            own(stage) if first else block(index, stage),
            block(index, stage),
            zs.at[stage, way, step],
            zr.at[stage, way, step],
            band=band(-2 if way else 2),
        )

    def pcopy(stage, k, first=False):
        index = band(2 * k)
        src = own(stage) if first else block(index, stage)
        return copy(src, block(index, stage), ps.at[stage, k], pr.at[stage, k], band=partner)

    def zstart(stage):
        zcopy(stage, 0, 0, True).start()
        if left_steps:
            zcopy(stage, 1, 0, True).start()
        pcopy(stage, 0, True).start()
        low, high = stages[stage]
        wall[pl.ds(pl.multiple_of(b * wrows, wrows), wrows), low:high] = w_ref[:, low:high]

    def zstep(stage, step):
        if isinstance(step, int):
            when = lambda condition: (lambda body: body() if condition else None)
        else:
            when = pl.when

        @when(step <= right_steps)
        def _():
            zcopy(stage, 0, step - 1).wait_recv()

            @when(step < right_steps)
            def _():
                zcopy(stage, 0, step).start()

            pcopy(stage, nz - step).start()

            @when(step <= left_steps)
            def _():
                zcopy(stage, 1, step - 1).wait_recv()

                @when(step < left_steps)
                def _():
                    zcopy(stage, 1, step).start()

                pcopy(stage, step).start()

    def zfinish(stage):
        for k in range(nz):
            pcopy(stage, k).wait_recv()
        for k in range(nz):
            pcopy(stage, k).wait_send()
        for way, steps in enumerate((right_steps, left_steps)):
            for step in range(steps):
                zcopy(stage, way, step).wait_send()

    longer = nh // 2
    shorter = nh - 1 - longer
    flows = ((1, 0, longer), (-1, 1, longer), (1, 1, shorter), (-1, 0, shorter))
    base = (0, longer, 2 * longer, 2 * longer + shorter)
    piece = share // GROUPS

    def share_rows(chunk, offset=0):
        return pl.ds(pl.multiple_of(offset + chunk * share, share), share)

    def piece_rows(chunk, group):
        return pl.ds(pl.multiple_of(chunk * share + group * piece, piece), piece)

    def half_of(half):
        return slice(half * half_cols, (half + 1) * half_cols)

    def rcopy(stage, group, flow, step):
        way, half, hops = flows[flow]
        slot = base[flow] + step
        return copy(
            p.at[stage % 2, piece_rows(head(way * (hops - step)), group), half_of(half)],
            slots.at[group, slot],
            rss.at[stage, group, slot],
            rsr.at[stage, group, slot],
            head=head(way),
        )

    def acopy(stage, group, flow, step):
        way, half, hops = flows[flow]
        slot = base[flow] + step
        view = x.at[piece_rows(head(-way * step), group), half_of(half)]
        return copy(
            view, view, ags.at[stage, group, slot], agr.at[stage, group, slot], head=head(way)
        )

    def scattered(stage, produce, ticks):
        @pl.loop(0, longer)
        def _(i):
            produce(i)
            for group in range(GROUPS):
                for flow, (way, half, hops) in enumerate(flows):
                    lag = longer - hops

                    def go(group=group, flow=flow, way=way, half=half, hops=hops, lag=lag):
                        step = i - lag

                        @pl.when(step > 0)
                        def _():
                            rcopy(stage, group, flow, step - 1).wait_recv()
                            where = piece_rows(head(way * (hops - step)), group)
                            p[stage % 2, where, half_of(half)] = (
                                p[stage % 2, where, half_of(half)].astype(jnp.float32)
                                + slots[group, base[flow] + step - 1].astype(jnp.float32)
                            ).astype(jnp.bfloat16)

                        rcopy(stage, group, flow, step).start()

                    if lag:
                        pl.when(i >= lag)(go)
                    else:
                        go()
            for z_stage, first in ticks:
                zstep(z_stage, first + i)

    def summed(stage, group):
        halves = [
            p[stage % 2, piece_rows(h, group), half_of(half)].astype(jnp.float32)
            for half in range(2)
        ]
        for flow, (way, half, hops) in enumerate(flows):
            rcopy(stage, group, flow, hops - 1).wait_recv()
            halves[half] = halves[half] + slots[group, base[flow] + hops - 1].astype(jnp.float32)
        return jnp.concatenate(halves, axis=1)

    def spread(stage, group, step):
        for flow, (way, half, hops) in enumerate(flows):
            if 1 <= step <= hops:
                acopy(stage, group, flow, step - 1).wait_recv()
            if step < hops:
                acopy(stage, group, flow, step).start()

    def settled(stage, with_gather=True):
        for group in range(GROUPS):
            for flow, (way, half, hops) in enumerate(flows):
                for step in range(hops):
                    rcopy(stage, group, flow, step).wait_send()
                    if with_gather:
                        acopy(stage, group, flow, step).wait_send()

    def arrived(step):
        if step == 0:
            return [h]
        if step <= shorter:
            return [head(-step), head(step)]
        return [head(step)]

    def rows_at(step):
        return jnp.concatenate([x[share_rows(c), :] for c in arrived(step)], axis=0)

    def finish(stage, residual, events):
        for group in range(GROUPS):
            state_rows = pl.ds(group * piece, piece)
            total = summed(stage, group) + residual(group)
            state[state_rows, :] = total
            x[piece_rows(h, group), :] = normed(total)
            spread(stage, group, 0)
        events(0)
        for step in range(1, longer + 1):
            for group in range(GROUPS):
                spread(stage, group, step)
            events(step)
        settled(stage)

    tile = min(256, rows)
    tiles = rows // tile

    def tile_rows(index, offset=0):
        return pl.ds(pl.multiple_of(offset + index * tile, tile), tile)

    def for_tiles(body):
        @pl.loop(0, tiles)
        def _(index):
            body(index)

    def norm_rows(src, dst):
        some = min(64, rows)

        @pl.loop(0, rows // some)
        def _(index):
            where = pl.ds(pl.multiple_of(index * some, some), some)
            dst[where, :] = normed(src[where, :].astype(jnp.float32))

    def project_q(stage, src):
        low = stages[stage][0]

        def body(index):
            q[tile_rows(index), :] = jnp.dot(
                src[tile_rows(index), :], wall[:, low : low + width], preferred_element_type=jnp.float32
            ).astype(jnp.bfloat16)

        for_tiles(body)

    def project_kv(stage, src, slab, offset):
        low = stages[stage][0]

        def body(index):
            slab[tile_rows(index, offset), :] = jnp.dot(
                src[tile_rows(index), :],
                wall[:, low + width : low + 3 * width],
                preferred_element_type=jnp.float32,
            ).astype(jnp.bfloat16)

        for_tiles(body)

    blocks = rows // BLOCK

    def block_at(i):
        farthest = lax.rem(h + nh // 2, nh) // (BLOCK // share)
        away = (i + 1) // 2 * (1 - 2 * lax.rem(i, 2)) * (1 - 2 * lax.rem(h, 2))
        return lax.rem(farthest + away + blocks, blocks)

    def attend(stage, index, slab, mask, keys, moving):
        lane = lax.broadcasted_iota(jnp.int32, (BLOCK, width), 1)
        where = pl.ds(pl.multiple_of(index * BLOCK, BLOCK), BLOCK)
        taken = pl.ds(pl.multiple_of(index * BLOCK, BLOCK), keys) if moving else pl.ds(0, keys)
        query = q[where, :]
        zero = jnp.zeros_like(query)
        both = jnp.concatenate(
            [jnp.where(lane < HD, query, zero), jnp.where(lane < HD, zero, query)], axis=0
        )
        scores = mask(contract_rows(both, slab[taken, 0:width]), index, where, taken)
        maxima = jnp.max(scores, axis=1, keepdims=True)
        expo = jnp.exp2((scores - maxima) * SCALE)
        totals = jnp.sum(expo, axis=1, keepdims=True)
        mixed = jnp.dot(
            expo.astype(jnp.bfloat16),
            slab[taken, width : 2 * width],
            preferred_element_type=jnp.float32,
        )
        mixed = mixed / totals
        mixed = jnp.where(lane < HD, mixed[:BLOCK], mixed[BLOCK:]).astype(jnp.bfloat16)
        low = stages[stage][0] + 3 * width
        p[stage % 2 if stage < 2 else 1, where, :] = contract_rows(
            mixed, wall[:, low : low + width]
        ).astype(jnp.bfloat16)

    def listed_mask(bias):
        def mask(scores, index, where, taken):
            return scores + bias[pl.ds(index, 1), :]

        return mask

    def window_mask(scores, index, where, taken):
        ids = query_ids[where, :]
        same = jnp.concatenate([ids, ids], axis=0) == key_ids[:, taken]
        return jnp.where(same, scores, NEGATIVE)

    def side(slab, o, first, where=None):
        k = 0 if o == 1 else 1
        start, count = (0, rows) if where is None else where
        return copy(
            slab.at[pl.ds(pl.multiple_of(rows + start, share), count), :],
            slab.at[pl.ds(pl.multiple_of((1 - o) * rows + start, share), count), :],
            hs.at[first + k],
            hr.at[first + k],
            band=band(o),
        )

    zstart(0)
    norm_rows(mesh_ref, x)
    zstep(0, 1)
    norm_rows(grid_ref, gn)
    for step in range(2, right_steps + 1):
        zstep(0, step)
    zfinish(0)
    project_kv(0, gn, eslab, rows)
    for o in (1, -1):
        side(eslab, o, 0).start()
    zstart(1)
    project_q(0, x)
    zstep(1, 1)
    for o in (1, -1):
        side(eslab, o, 0).wait_recv()
    zstep(1, 2)

    def encode(i):
        attend(0, block_at(i), eslab, listed_mask(enc_bias), 3 * rows, False)

    scattered(0, encode, ((1, 3),))

    def mesh_rows(group):
        return mesh_ref[piece_rows(h, group), :].astype(jnp.float32)

    def state_rows(group):
        return state[pl.ds(group * piece, piece), :]

    def part(place, where=None):
        start, count = (0, rows) if where is None else where
        return wslab.at[pl.ds(pl.multiple_of(place * rows + start, share), count), :]

    def window_moves(where=None):
        view = part(REACH, where)
        far = lax.rem(b + 6 * odd - 3 + nb, nb)
        return (
            copy(view, part(1, where), hs.at[2], hr.at[2], band=band(2)),
            copy(view, part(5, where), hs.at[3], hr.at[3], band=band(-2)),
            copy(view, part(6 - 6 * odd, where), hs.at[5], hr.at[5], band=far),
            copy(view, part(2 + 2 * odd, where), hs.at[4], hr.at[4], band=partner),
        )

    def proc_rows(step):
        low = stages[1][0]
        made = jnp.dot(
            rows_at(step), wall[:, low : low + 3 * width], preferred_element_type=jnp.float32
        ).astype(jnp.bfloat16)
        for k, chunk in enumerate(arrived(step)):
            mine = made[k * share : (k + 1) * share]
            q[share_rows(chunk), :] = mine[:, :width]
            wslab[share_rows(chunk, REACH * rows), :] = mine[:, width:]
            for move in window_moves((chunk * share, share)):
                move.start()

    def after_encoder(step):
        if step == 0:
            zstep(1, longer + 3)
            return
        if step == 1:
            for late in range(longer + 4, right_steps + 1):
                zstep(1, late)
            zfinish(1)
            proc_rows(0)
        proc_rows(step)

    finish(0, mesh_rows, after_encoder)

    zstart(2)
    moves = window_moves()
    passed = (
        copy(part(1), part(2 * odd), hs.at[6], hr.at[6], band=partner),
        copy(part(5), part(4 + 2 * odd), hs.at[7], hr.at[7], band=partner),
    )
    for move, onward in zip(moves, passed):
        move.wait_recv()
        onward.start()
    zstep(2, 1)
    for move in (moves[3], moves[2], *passed):
        move.wait_recv()

    def process(i):
        attend(1, block_at(i), wslab, window_mask, 2 * REACH * rows + BLOCK, True)

    scattered(1, process, ((2, 2),))

    def after_processor(step):
        if step == 0:
            zstart(3)
        else:
            zstep(3, step)
        zstep(2, longer + 2 + step)

    finish(1, state_rows, after_processor)
    for late in range(2 * longer + 3, right_steps + 1):
        zstep(2, late)
    zfinish(2)

    def feed(i):
        low = stages[2][0]
        where = pl.ds(pl.multiple_of(block_at(i) * BLOCK, BLOCK), BLOCK)
        inner = jnp.dot(x[where, :], wall[:, low : low + ff], preferred_element_type=jnp.float32)
        hidden = (inner * 0.5 * (1.0 + lax.erf(inner * 0.5**0.5))).astype(jnp.bfloat16)
        p[0, where, :] = contract_rows(hidden, wall[:, low + ff : low + 2 * ff]).astype(jnp.bfloat16)

    scattered(2, feed, ((3, longer + 1),))
    for late in range(2 * longer + 1, right_steps + 1):
        zstep(3, late)
    zfinish(3)

    def dec_rows(step):
        low = stages[3][0]
        made = jnp.dot(
            rows_at(step), wall[:, low + width : low + 3 * width], preferred_element_type=jnp.float32
        ).astype(jnp.bfloat16)
        for k, chunk in enumerate(arrived(step)):
            dslab[share_rows(chunk, rows), :] = made[k * share : (k + 1) * share]
            for o in (1, -1):
                side(dslab, o, 8, (chunk * share, share)).start()

    finish(2, state_rows, dec_rows)

    project_q(3, gn)
    for o in (1, -1):
        side(dslab, o, 8).wait_recv()

    def decode(i):
        attend(3, block_at(i), dslab, listed_mask(dec_bias), 3 * rows, False)

    scattered(3, decode, ())
    for group in range(GROUPS):
        residual = grid_ref[piece_rows(h, group), :].astype(jnp.float32)
        out_ref[pl.ds(group * piece, piece), :] = (residual + summed(3, group)).astype(jnp.bfloat16)
    settled(3, False)
    for o in (1, -1):
        side(eslab, o, 0).wait_send()
        side(dslab, o, 8).wait_send()
    for move in (*moves, *passed):
        move.wait_send()


def listed_bias(lists, counts, b, blocks, keys_per_block):
    my_lists = lax.dynamic_slice_in_dim(lists, b * blocks, blocks, 0) - (b - 1) * keys_per_block
    my_counts = lax.dynamic_slice_in_dim(counts, b * blocks, blocks, 0)
    live = jnp.arange(lists.shape[1], dtype=jnp.int32)[None, :] < my_counts[:, None]
    places = jnp.arange(3 * keys_per_block * BLOCK, dtype=jnp.int32) // BLOCK
    hit = (my_lists[:, :, None] == places[None, None, :]) & live[:, :, None]
    return jnp.where(jnp.any(hit, axis=1), 0.0, NEGATIVE).astype(jnp.float32)


def per_device(
    nb,
    nh,
    grid_feats,
    mesh_feats,
    enc_in,
    enc_out,
    proc_in,
    proc_out,
    ff_up,
    ff_down,
    dec_in,
    dec_out,
    enc_list,
    enc_count,
    dec_list,
    dec_count,
    window_ids,
):
    b = lax.axis_index("band")
    rows, depth = mesh_feats.shape
    assert grid_feats.shape == mesh_feats.shape and WINDOW <= REACH * rows
    assert nh == rows // BLOCK * 2
    width = enc_in.shape[2]
    ff = ff_up.shape[1]
    share = rows // nh
    nz = nb // 2
    w = jnp.concatenate(
        [
            *(enc_in[k] for k in range(3)),
            enc_out.T,
            *(proc_in[k] for k in range(3)),
            proc_out.T,
            ff_up,
            ff_down.T,
            *(dec_in[k] for k in range(3)),
            dec_out.T,
        ],
        axis=1,
    )
    blocks = rows // BLOCK
    enc_bias = listed_bias(enc_list, enc_count, b, blocks, blocks)
    dec_bias = listed_bias(dec_list, dec_count, b, blocks, blocks)
    padded = jnp.pad(window_ids, (REACH * rows, REACH * rows), constant_values=-1)
    key_ids = lax.dynamic_slice_in_dim(padded, b * rows, (2 * REACH + 1) * rows, 0)[None, :]
    query_ids = lax.dynamic_slice_in_dim(window_ids, b * rows, rows, 0)[:, None]
    bf16, f32 = jnp.bfloat16, jnp.float32
    dma = pltpu.SemaphoreType.DMA
    msgs = 2 * (nh - 1)
    vmem = pl.BlockSpec(memory_space=pltpu.VMEM)
    return pl.pallas_call(
        functools.partial(kernel, nb, nh),
        out_shape=jax.ShapeDtypeStruct((share, depth), bf16),
        in_specs=[vmem] * 7,
        out_specs=vmem,
        scratch_shapes=[
            pltpu.VMEM((nb * w.shape[0], w.shape[1]), bf16),
            pltpu.VMEM((rows, depth), bf16),
            pltpu.VMEM((rows, depth), bf16),
            pltpu.VMEM((rows, width), bf16),
            pltpu.VMEM((2, rows, depth), bf16),
            pltpu.VMEM((GROUPS, msgs, share // GROUPS, depth // 2), bf16),
            pltpu.VMEM((3 * rows, 2 * width), bf16),
            pltpu.VMEM(((2 * REACH + 1) * rows, 2 * width), bf16),
            pltpu.VMEM((3 * rows, 2 * width), bf16),
            pltpu.VMEM((share, depth), f32),
            dma((4, 2, nz // 2)),
            dma((4, 2, nz // 2)),
            dma((4, nz)),
            dma((4, nz)),
            dma((4, GROUPS, msgs)),
            dma((4, GROUPS, msgs)),
            dma((3, GROUPS, msgs)),
            dma((3, GROUPS, msgs)),
            dma((10,)),
            dma((10,)),
        ],
        compiler_params=pltpu.CompilerParams(
            collective_id=0, has_side_effects=True, vmem_limit_bytes=60 * 1024 * 1024
        ),
    )(grid_feats, mesh_feats, w, enc_bias, dec_bias, key_ids, query_ids)


def solution(mesh):
    rows = P(("members", "band"), None)
    placed = (
        rows,
        rows,
        P(None, "band", "head"),
        P("head", "band"),
        P(None, "band", "head"),
        P("head", "band"),
        P("band", "head"),
        P("head", "band"),
        P(None, "band", "head"),
        P("head", "band"),
        P(),
        P(),
        P(),
        P(),
        P(),
    )
    return jax.shard_map(
        functools.partial(per_device, mesh.shape["band"], mesh.shape["head"]),
        mesh=mesh,
        in_specs=placed,
        out_specs=P(("members", "band", "head"), None),
        check_vma=False,
    )
```

time: 238 us -> 221 us (0.929)
  Pallas kernels: 225 us -> 209 us
    pallas_call x1, Pallas kernels: 225 us -> 209 us  [per_device(): pl.pallas_call(functools.partial(kernel, nb, nh), out_shape=jax.ShapeDtyp...]
where the time goes in v2:
time: 221 us
  Pallas kernels  209 us (95%)
  local copies, waits for them, and re-layouts  9.23 us (4%)
  other arithmetic  2.32 us (1%)
    pallas_call x1, Pallas kernels, per_device(): pl.pallas_call(functools.partial(kernel, nb, nh), out_shape=jax.ShapeDtyp...  209 us
    unnamed x34, local copies, waits for them, and re-layouts  5.26 us

profile of v2, /device:TPU:65, one launch (start us, length us, event | category | flops | bytes accessed | tf_op | source)
XLA Modules:
  0.0 220.9 jit_solution(3518322020069851361)
XLA Ops:
  0.0 0.0 copy-start.1
  0.0 0.8 dynamic_slice.19
  0.8 0.7 dynamic_slice.21
  1.5 0.1 iota_compare_fusion
  1.6 0.8 dynamic_slice.23
  2.3 0.8 dynamic-slice_subtract_fusion
  3.1 0.1 copy.22
  3.2 0.1 copy.21
  3.3 0.2 and_reduce_fusion
  3.5 0.0 copy-done.1
  3.5 0.1 pad_dynamic-slice_fusion
  3.6 0.6 broadcast_in_dim.28.key_ids
  4.2 0.0 copy-start.4
  4.2 0.6 broadcast_select_fusion.dec_bias
  4.8 0.6 broadcast_select_fusion.1.enc_bias
  5.5 0.0 copy-done.4
  5.5 0.0 copy-start.5
  5.5 0.0 copy-start.7
  5.5 0.7 copy-done.7
  6.2 0.0 copy-done.5
  6.2 0.0 copy-start.2
  6.2 0.0 copy-start.8
  6.2 0.7 copy-done.8
  6.9 0.0 copy-done.2
  7.0 0.0 copy-start.3
  7.0 0.8 copy-done.3
  7.7 0.0 copy-start.6
  7.7 0.7 copy-done.6
  8.5 0.0 copy-start.9
  8.5 0.7 copy-done.9
  9.2 0.0 copy-start
  9.2 0.9 copy.23.query_ids
  10.0 0.0 copy-done
  10.0 209.2 %shard_map.145 = bf16[64,1024]{1,0:T(8,128)(2,1)} custom-call(bf16[512,1024]{1,0:T(8,128)(2,1)} %grid_ref.1, bf16[512,1024]{1,0:T(8,128)(2,1)} %mesh_ref.1, bf16[32,2560]{1,0:T(8,128)(2,1)} %copy-done, f32[4,1536]{1,0:T(4,128)} %broadcast_select_fusion.1.enc_bias, f32[4,1536]{1,0:T(4,128)} %broadcast_select_fusion.dec_bias, ...), custom_call_target="tpu_custom_call" | custom-call | tf_op jit(solution)/shard_map/pallas_call | solution.py:579
  219.3 1.6 copy.38
  (15 shorter events, 0.1 us)
Async XLA Ops:
  0.0 3.5 %copy-start.1 = (s32[16384]{0:T(1024)S(1)}, s32[16384]{0:T(1024)}, u32[]{:S(2)}) copy-start(s32[16384]{0:T(1024)} %param.29) | copy-start | bytes 196612
  4.2 1.2 copy-start.4
  5.5 0.7 copy-start.5
  5.5 0.7 copy-start.7
  6.2 0.8 copy-start.2
  6.2 0.7 copy-start.8
  7.0 0.8 copy-start.3
  7.7 0.7 copy-start.6
  8.5 0.7 copy-start.9
  9.2 0.9 copy-start

commit v3 on v2

--- a/solution.py
+++ b/solution.py
@@ -33,11 +33,19 @@
     nh,
     grid_ref,
     mesh_ref,
-    w_ref,
-    enc_bias,
-    dec_bias,
-    key_ids,
-    query_ids,
+    enc_in,
+    enc_out,
+    proc_in,
+    proc_out,
+    ff_up,
+    ff_down,
+    dec_in,
+    dec_out,
+    enc_list,
+    enc_count,
+    dec_list,
+    dec_count,
+    ids,
     out_ref,
     wall,
     x,
@@ -49,9 +57,12 @@
     wslab,
     dslab,
     state,
+    enc_bias,
+    dec_bias,
+    key_ids,
+    query_ids,
     zs,
     zr,
-    ps,
     pr,
     rss,
     rsr,
@@ -64,10 +75,10 @@
     h = lax.axis_index("head")
     rows, depth = grid_ref.shape
     width = q.shape[1]
-    ff = (w_ref.shape[1] - 12 * width) // 2
+    ff = ff_up.shape[1]
     share = rows // nh
     half_cols = depth // 2
-    wrows = w_ref.shape[0]
+    wrows = ff_up.shape[0]
     nz = nb // 2
     odd = lax.rem(b, 2)
     partner = b + 1 - 2 * odd
@@ -94,81 +105,88 @@
             device_id_type=MESH_ID,
         )
 
+    place = 0
+    own_rows = pl.ds(pl.multiple_of(b * wrows, wrows), wrows)
+    for three, out in ((enc_in, enc_out), (proc_in, proc_out), (ff_up, ff_down), (dec_in, dec_out)):
+        pieces = [three[k] for k in range(3)] if len(three.shape) == 3 else [three[...]]
+        for one in (*pieces, out[...]):
+            wall[own_rows, place : place + one.shape[1]] = one
+            place += one.shape[1]
+
     barrier = pltpu.get_barrier_semaphore()
-    peers = [{"band": band(o), "head": h} for o in (1, -1, 2, -2, 3, -3)]
+    peers = [{"band": band(o), "head": h} for o in (1, -1, 2, -2, 3, -3, 4, -4)]
     peers += [{"band": b, "head": head(o)} for o in (1, -1)]
     for peer in peers:
         pl.semaphore_signal(barrier, inc=1, device_id=peer, device_id_type=MESH_ID)
     pl.semaphore_wait(barrier, len(peers))
 
-    right_steps = nz // 2
-    left_steps = nz - 1 - right_steps
-
-    def block(index, stage):
+    reaches = (nz // 2, nz - 1 - nz // 2)
+    z_steps = (reaches[0] + 1) // 2
+
+    def wall_rows(start, count, stage):
         low, high = stages[stage]
-        return wall.at[pl.ds(pl.multiple_of(index * wrows, wrows), wrows), low:high]
-
-    def own(stage):
-        low, high = stages[stage]
-        return w_ref.at[:, low:high]
-
-    def zcopy(stage, way, step, first=False):
-        index = band(2 * step if way else -2 * step)
+        return wall.at[pl.ds(pl.multiple_of(start * wrows, wrows), count * wrows), low:high]
+
+    def zcopy(stage, way, near, step):
+        side_of = -1 if way else 1
+        view = wall_rows(band(-4 * side_of * step), 1, stage)
         return copy(
-            own(stage) if first else block(index, stage),
-            block(index, stage),
-            zs.at[stage, way, step],
-            zr.at[stage, way, step],
-            band=band(-2 if way else 2),
-        )
-
-    def pcopy(stage, k, first=False):
-        index = band(2 * k)
-        src = own(stage) if first else block(index, stage)
-        return copy(src, block(index, stage), ps.at[stage, k], pr.at[stage, k], band=partner)
+            view,
+            view,
+            zs.at[stage],
+            zr.at[stage, way, near, step],
+            band=band(side_of * (2 if near else 4)),
+        )
+
+    def hand_over(stage, way, distance):
+        view = wall_rows(band(2 * distance if way else -2 * distance), 1, stage)
+        copy(view, view, zs.at[stage], pr.at[stage], band=partner).start()
 
     def zstart(stage):
-        zcopy(stage, 0, 0, True).start()
-        if left_steps:
-            zcopy(stage, 1, 0, True).start()
-        pcopy(stage, 0, True).start()
-        low, high = stages[stage]
-        wall[pl.ds(pl.multiple_of(b * wrows, wrows), wrows), low:high] = w_ref[:, low:high]
+        for way, reach in enumerate(reaches):
+            if reach >= 2:
+                zcopy(stage, way, 0, 0).start()
+            if reach >= 1:
+                zcopy(stage, way, 1, 0).start()
+        hand_over(stage, 0, 0)
 
     def zstep(stage, step):
         if isinstance(step, int):
             when = lambda condition: (lambda body: body() if condition else None)
         else:
             when = pl.when
-
-        @when(step <= right_steps)
-        def _():
-            zcopy(stage, 0, step - 1).wait_recv()
-
-            @when(step < right_steps)
-            def _():
-                zcopy(stage, 0, step).start()
-
-            pcopy(stage, nz - step).start()
-
-            @when(step <= left_steps)
-            def _():
-                zcopy(stage, 1, step - 1).wait_recv()
-
-                @when(step < left_steps)
+        for way, reach in enumerate(reaches):
+
+            @when(2 * step <= reach)
+            def _(way=way, reach=reach):
+                zcopy(stage, way, 0, step - 1).wait_recv()
+
+                @when(2 * step + 2 <= reach)
                 def _():
-                    zcopy(stage, 1, step).start()
-
-                pcopy(stage, step).start()
+                    zcopy(stage, way, 0, step).start()
+
+                @when(2 * step + 1 <= reach)
+                def _():
+                    zcopy(stage, way, 1, step).start()
+
+        for way, reach in enumerate(reaches):
+
+            @when(2 * step <= reach)
+            def _(way=way):
+                hand_over(stage, way, 2 * step)
+
+            @when(2 * step - 1 <= reach)
+            def _(way=way):
+                zcopy(stage, way, 1, step - 1).wait_recv()
+                hand_over(stage, way, 2 * step - 1)
 
     def zfinish(stage):
-        for k in range(nz):
-            pcopy(stage, k).wait_recv()
-        for k in range(nz):
-            pcopy(stage, k).wait_send()
-        for way, steps in enumerate((right_steps, left_steps)):
-            for step in range(steps):
-                zcopy(stage, way, step).wait_send()
+        whole = wall_rows(0, nz, stage)
+        copy(whole, whole, zs.at[stage], pr.at[stage]).wait_recv()
+
+    def zsettle(stage):
+        whole = wall_rows(0, 2 * nz - 1, stage)
+        copy(whole, whole, zs.at[stage], pr.at[stage]).wait_send()
 
     longer = nh // 2
     shorter = nh - 1 - longer
@@ -191,8 +209,8 @@
         return copy(
             p.at[stage % 2, piece_rows(head(way * (hops - step)), group), half_of(half)],
             slots.at[group, slot],
-            rss.at[stage, group, slot],
-            rsr.at[stage, group, slot],
+            rss.at[0],
+            rsr.at[group, slot],
             head=head(way),
         )
 
@@ -200,9 +218,7 @@
         way, half, hops = flows[flow]
         slot = base[flow] + step
         view = x.at[piece_rows(head(-way * step), group), half_of(half)]
-        return copy(
-            view, view, ags.at[stage, group, slot], agr.at[stage, group, slot], head=head(way)
-        )
+        return copy(view, view, ags.at[0], agr.at[group, slot], head=head(way))
 
     def scattered(stage, produce, ticks):
         @pl.loop(0, longer)
@@ -231,7 +247,10 @@
                     else:
                         go()
             for z_stage, first in ticks:
-                zstep(z_stage, first + i)
+
+                @pl.when(lax.rem(i, 2) == 1)
+                def _(z_stage=z_stage, first=first):
+                    zstep(z_stage, first + i // 2)
 
     def summed(stage, group):
         halves = [
@@ -250,13 +269,10 @@
             if step < hops:
                 acopy(stage, group, flow, step).start()
 
-    def settled(stage, with_gather=True):
-        for group in range(GROUPS):
-            for flow, (way, half, hops) in enumerate(flows):
-                for step in range(hops):
-                    rcopy(stage, group, flow, step).wait_send()
-                    if with_gather:
-                        acopy(stage, group, flow, step).wait_send()
+    def settled(with_gather=True):
+        copy(slots, slots, rss.at[0], rsr.at[0, 0]).wait_send()
+        if with_gather:
+            copy(slots, slots, ags.at[0], agr.at[0, 0]).wait_send()
 
     def arrived(step):
         if step == 0:
@@ -280,7 +296,7 @@
             for group in range(GROUPS):
                 spread(stage, group, step)
             events(step)
-        settled(stage)
+        settled()
 
     tile = min(256, rows)
     tiles = rows // tile
@@ -377,27 +393,66 @@
             band=band(o),
         )
 
+    def fill_bias(lists, counts, bias):
+        lane = lax.broadcasted_iota(jnp.int32, lists.shape, 1)
+        slot = lax.broadcasted_iota(jnp.int32, (lists.shape[0], 1), 0).astype(jnp.float32)
+        places = lax.broadcasted_iota(jnp.int32, (lists.shape[0], 3 * rows), 1)
+        places = lax.shift_right_logical(places, BLOCK.bit_length() - 1).astype(jnp.float32)
+        listed = lists[...].astype(jnp.float32)
+        counted = counts[...].astype(jnp.float32)
+        first = ((b - 1) * blocks).astype(jnp.float32)
+        for index in range(blocks):
+            mine = lane == b * blocks + index
+            picked = jnp.sum(jnp.where(mine, listed, 0.0), axis=1, keepdims=True)
+            count = jnp.sum(jnp.where(mine[:1], counted, 0.0), axis=1, keepdims=True)
+            local = jnp.where(slot < count, picked - first, -1.0)
+            hits = jnp.where(local == places, 0.0, NEGATIVE)
+            bias[index : index + 1, :] = jnp.max(hits, axis=0, keepdims=True)
+
+    def fill_ids():
+        total = ids.shape[0]
+        for k in range((2 * REACH + 1) * blocks):
+            row = (b - REACH) * blocks + k
+            inside = ((row >= 0) & (row < total)).astype(jnp.int32)
+            found = ids[pl.ds(lax.rem(row + total, total), 1), :]
+            key_ids[:, k * BLOCK : (k + 1) * BLOCK] = (found * inside + (inside - 1)).astype(
+                jnp.float32
+            )
+        diagonal = lax.broadcasted_iota(jnp.int32, (BLOCK, BLOCK), 0) == lax.broadcasted_iota(
+            jnp.int32, (BLOCK, BLOCK), 1
+        )
+        for k in range(blocks):
+            row = key_ids[:, (REACH * blocks + k) * BLOCK : (REACH * blocks + k + 1) * BLOCK]
+            query_ids[k * BLOCK : (k + 1) * BLOCK, :] = jnp.sum(
+                jnp.where(diagonal, row, 0.0), axis=1, keepdims=True
+            )
+
     zstart(0)
+    zstart(1)
     norm_rows(mesh_ref, x)
-    zstep(0, 1)
-    norm_rows(grid_ref, gn)
-    for step in range(2, right_steps + 1):
+    fill_bias(enc_list, enc_count, enc_bias)
+    fill_bias(dec_list, dec_count, dec_bias)
+    for step in range(1, z_steps + 1):
         zstep(0, step)
+        if step == 1:
+            norm_rows(grid_ref, gn)
+            fill_ids()
+        if step < z_steps:
+            zstep(1, step)
     zfinish(0)
     project_kv(0, gn, eslab, rows)
     for o in (1, -1):
         side(eslab, o, 0).start()
-    zstart(1)
     project_q(0, x)
-    zstep(1, 1)
     for o in (1, -1):
         side(eslab, o, 0).wait_recv()
-    zstep(1, 2)
 
     def encode(i):
         attend(0, block_at(i), eslab, listed_mask(enc_bias), 3 * rows, False)
 
-    scattered(0, encode, ((1, 3),))
+    scattered(0, encode, ())
+    zstep(1, z_steps)
+    zfinish(1)
 
     def mesh_rows(group):
         return mesh_ref[piece_rows(h, group), :].astype(jnp.float32)
@@ -431,18 +486,7 @@
             for move in window_moves((chunk * share, share)):
                 move.start()
 
-    def after_encoder(step):
-        if step == 0:
-            zstep(1, longer + 3)
-            return
-        if step == 1:
-            for late in range(longer + 4, right_steps + 1):
-                zstep(1, late)
-            zfinish(1)
-            proc_rows(0)
-        proc_rows(step)
-
-    finish(0, mesh_rows, after_encoder)
+    finish(0, mesh_rows, proc_rows)
 
     zstart(2)
     moves = window_moves()
@@ -453,25 +497,23 @@
     for move, onward in zip(moves, passed):
         move.wait_recv()
         onward.start()
-    zstep(2, 1)
     for move in (moves[3], moves[2], *passed):
         move.wait_recv()
 
     def process(i):
         attend(1, block_at(i), wslab, window_mask, 2 * REACH * rows + BLOCK, True)
 
-    scattered(1, process, ((2, 2),))
+    scattered(1, process, ((2, 1),))
 
     def after_processor(step):
         if step == 0:
             zstart(3)
+        elif step % 2:
+            zstep(2, longer // 2 + (step + 1) // 2)
         else:
-            zstep(3, step)
-        zstep(2, longer + 2 + step)
+            zstep(3, step // 2)
 
     finish(1, state_rows, after_processor)
-    for late in range(2 * longer + 3, right_steps + 1):
-        zstep(2, late)
     zfinish(2)
 
     def feed(i):
@@ -481,9 +523,7 @@
         hidden = (inner * 0.5 * (1.0 + lax.erf(inner * 0.5**0.5))).astype(jnp.bfloat16)
         p[0, where, :] = contract_rows(hidden, wall[:, low + ff : low + 2 * ff]).astype(jnp.bfloat16)
 
-    scattered(2, feed, ((3, longer + 1),))
-    for late in range(2 * longer + 1, right_steps + 1):
-        zstep(3, late)
+    scattered(2, feed, ((3, longer // 2 + 1),))
     zfinish(3)
 
     def dec_rows(step):
@@ -509,21 +549,14 @@
     for group in range(GROUPS):
         residual = grid_ref[piece_rows(h, group), :].astype(jnp.float32)
         out_ref[pl.ds(group * piece, piece), :] = (residual + summed(3, group)).astype(jnp.bfloat16)
-    settled(3, False)
+    settled(False)
     for o in (1, -1):
         side(eslab, o, 0).wait_send()
         side(dslab, o, 8).wait_send()
     for move in (*moves, *passed):
         move.wait_send()
-
-
-def listed_bias(lists, counts, b, blocks, keys_per_block):
-    my_lists = lax.dynamic_slice_in_dim(lists, b * blocks, blocks, 0) - (b - 1) * keys_per_block
-    my_counts = lax.dynamic_slice_in_dim(counts, b * blocks, blocks, 0)
-    live = jnp.arange(lists.shape[1], dtype=jnp.int32)[None, :] < my_counts[:, None]
-    places = jnp.arange(3 * keys_per_block * BLOCK, dtype=jnp.int32) // BLOCK
-    hit = (my_lists[:, :, None] == places[None, None, :]) & live[:, :, None]
-    return jnp.where(jnp.any(hit, axis=1), 0.0, NEGATIVE).astype(jnp.float32)
+    for stage in range(4):
+        zsettle(stage)
 
 
 def per_device(
@@ -545,33 +578,31 @@
     dec_count,
     window_ids,
 ):
-    b = lax.axis_index("band")
     rows, depth = mesh_feats.shape
     assert grid_feats.shape == mesh_feats.shape and WINDOW <= REACH * rows
     assert nh == rows // BLOCK * 2
     width = enc_in.shape[2]
-    ff = ff_up.shape[1]
+    wrows, ff = ff_up.shape
     share = rows // nh
     nz = nb // 2
-    w = jnp.concatenate(
-        [
-            *(enc_in[k] for k in range(3)),
-            enc_out.T,
-            *(proc_in[k] for k in range(3)),
-            proc_out.T,
-            ff_up,
-            ff_down.T,
-            *(dec_in[k] for k in range(3)),
-            dec_out.T,
-        ],
-        axis=1,
+    blocks = rows // BLOCK
+    given = (
+        grid_feats,
+        mesh_feats,
+        enc_in,
+        enc_out.T,
+        proc_in,
+        proc_out.T,
+        ff_up,
+        ff_down.T,
+        dec_in,
+        dec_out.T,
+        enc_list.T,
+        enc_count[None, :],
+        dec_list.T,
+        dec_count[None, :],
+        window_ids.reshape(-1, BLOCK),
     )
-    blocks = rows // BLOCK
-    enc_bias = listed_bias(enc_list, enc_count, b, blocks, blocks)
-    dec_bias = listed_bias(dec_list, dec_count, b, blocks, blocks)
-    padded = jnp.pad(window_ids, (REACH * rows, REACH * rows), constant_values=-1)
-    key_ids = lax.dynamic_slice_in_dim(padded, b * rows, (2 * REACH + 1) * rows, 0)[None, :]
-    query_ids = lax.dynamic_slice_in_dim(window_ids, b * rows, rows, 0)[:, None]
     bf16, f32 = jnp.bfloat16, jnp.float32
     dma = pltpu.SemaphoreType.DMA
     msgs = 2 * (nh - 1)
@@ -579,10 +610,10 @@
     return pl.pallas_call(
         functools.partial(kernel, nb, nh),
         out_shape=jax.ShapeDtypeStruct((share, depth), bf16),
-        in_specs=[vmem] * 7,
+        in_specs=[vmem] * len(given),
         out_specs=vmem,
         scratch_shapes=[
-            pltpu.VMEM((nb * w.shape[0], w.shape[1]), bf16),
+            pltpu.VMEM((nb * wrows, 12 * width + 2 * ff), bf16),
             pltpu.VMEM((rows, depth), bf16),
             pltpu.VMEM((rows, depth), bf16),
             pltpu.VMEM((rows, width), bf16),
@@ -592,21 +623,24 @@
             pltpu.VMEM(((2 * REACH + 1) * rows, 2 * width), bf16),
             pltpu.VMEM((3 * rows, 2 * width), bf16),
             pltpu.VMEM((share, depth), f32),
-            dma((4, 2, nz // 2)),
-            dma((4, 2, nz // 2)),
-            dma((4, nz)),
-            dma((4, nz)),
-            dma((4, GROUPS, msgs)),
-            dma((4, GROUPS, msgs)),
-            dma((3, GROUPS, msgs)),
-            dma((3, GROUPS, msgs)),
+            pltpu.VMEM((blocks, 3 * rows), f32),
+            pltpu.VMEM((blocks, 3 * rows), f32),
+            pltpu.VMEM((1, (2 * REACH + 1) * rows), f32),
+            pltpu.VMEM((rows, 1), f32),
+            dma((4,)),
+            dma((4, 2, 2, max(1, nz // 4))),
+            dma((4,)),
+            dma((1,)),
+            dma((GROUPS, msgs)),
+            dma((1,)),
+            dma((GROUPS, msgs)),
             dma((10,)),
             dma((10,)),
         ],
         compiler_params=pltpu.CompilerParams(
             collective_id=0, has_side_effects=True, vmem_limit_bytes=60 * 1024 * 1024
         ),
-    )(grid_feats, mesh_feats, w, enc_bias, dec_bias, key_ids, query_ids)
+    )(*given)
 
 
 def solution(mesh):

time: 221 us -> 194 us (0.88)
  Pallas kernels: 209 us -> 192 us
  local copies, waits for them, and re-layouts: 9.23 us -> 1.57 us
  other arithmetic: 2.32 us -> 0 us
    pallas_call x1, Pallas kernels: 209 us -> 192 us  [per_device(): pl.pallas_call(functools.partial(kernel, nb, nh), out_shape=jax.ShapeDtyp...]
    unnamed x34 -> x1, local copies, waits for them, and re-layouts: 5.26 us -> 1.57 us
    dynamic_slice x4 -> x0, local copies, waits for them, and re-layouts: 2.34 us -> none  [the longest x2 1.49 us: listed_bias(): my_counts = lax.dynamic_slice_in_dim(counts, b * blocks, blocks, 0)]
where the time goes in v3:
time: 194 us
  Pallas kernels  192 us (99%)
    pallas_call x1, Pallas kernels, per_device(): pl.pallas_call(functools.partial(kernel, nb, nh), out_shape=jax.ShapeDtyp...  192 us

profile of v3, /device:TPU:65, one launch (start us, length us, event | category | flops | bytes accessed | tf_op | source)
XLA Modules:
  0.0 193.8 jit_solution(565582365810344582)
XLA Ops:
  0.0 192.2 %shard_map.145 = bf16[64,1024]{1,0:T(8,128)(2,1)} custom-call(bf16[512,1024]{1,0:T(8,128)(2,1)} %grid_ref.1, bf16[512,1024]{1,0:T(8,128)(2,1)} %mesh_ref.1, bf16[3,32,128]{2,1,0:T(8,128)(2,1)} %enc_in.1, bf16[32,128]{1,0:T(8,128)(2,1)} %bitcast.11, bf16[3,32,128]{2,1,0:T(8,128)(2,1)} %proc_in.1, bf16[32,128]{1,0:T(8,128)(2,1)} %bitcast.12, ...), custom_call_target="tpu_custom_call" | custom-call | tf_op jit(solution)/shard_map/pallas_call | solution.py:610
  192.2 1.6 copy.17

commit v4 on v3

--- a/solution.py
+++ b/solution.py
@@ -11,7 +11,7 @@
 BLOCK = 128
 WINDOW = 1536
 REACH = 3
-GROUPS = 2
+GROUPS = 4
 EPSILON = 1e-05
 NEGATIVE = -1e30
 SCALE = HD ** (-0.5) * 1.4426950408889634

time: 194 us -> 192 us (0.990)
  Pallas kernels: 192 us -> 190 us
    pallas_call x1, Pallas kernels: 192 us -> 190 us  [per_device(): pl.pallas_call(functools.partial(kernel, nb, nh), out_shape=jax.ShapeDtyp...]
where the time goes in v4:
time: 192 us; the launch traced here: 191 us
  Pallas kernels  190 us (99%)
    pallas_call x1, Pallas kernels, per_device(): pl.pallas_call(functools.partial(kernel, nb, nh), out_shape=jax.ShapeDtyp...  190 us

profile of v4, /device:TPU:65, one launch (start us, length us, event | category | flops | bytes accessed | tf_op | source)
XLA Modules:
  0.0 191.5 jit_solution(2913284698446485117)
XLA Ops:
  0.0 189.9 %shard_map.145 = bf16[64,1024]{1,0:T(8,128)(2,1)} custom-call(bf16[512,1024]{1,0:T(8,128)(2,1)} %grid_ref.1, bf16[512,1024]{1,0:T(8,128)(2,1)} %mesh_ref.1, bf16[3,32,128]{2,1,0:T(8,128)(2,1)} %enc_in.1, bf16[32,128]{1,0:T(8,128)(2,1)} %bitcast.11, bf16[3,32,128]{2,1,0:T(8,128)(2,1)} %proc_in.1, bf16[32,128]{1,0:T(8,128)(2,1)} %bitcast.12, ...), custom_call_target="tpu_custom_call" | custom-call | tf_op jit(solution)/shard_map/pallas_call | solution.py:610
  189.9 1.6 copy.17

commit v5 on v4

--- a/solution.py
+++ b/solution.py
@@ -221,36 +221,46 @@
         return copy(view, view, ags.at[0], agr.at[group, slot], head=head(way))
 
     def scattered(stage, produce, ticks):
-        @pl.loop(0, longer)
+        @pl.loop(0, longer + 1)
         def _(i):
-            produce(i)
-            for group in range(GROUPS):
-                for flow, (way, half, hops) in enumerate(flows):
-                    lag = longer - hops
-
-                    def go(group=group, flow=flow, way=way, half=half, hops=hops, lag=lag):
-                        step = i - lag
-
-                        @pl.when(step > 0)
-                        def _():
-                            rcopy(stage, group, flow, step - 1).wait_recv()
-                            where = piece_rows(head(way * (hops - step)), group)
-                            p[stage % 2, where, half_of(half)] = (
-                                p[stage % 2, where, half_of(half)].astype(jnp.float32)
-                                + slots[group, base[flow] + step - 1].astype(jnp.float32)
-                            ).astype(jnp.bfloat16)
-
-                        rcopy(stage, group, flow, step).start()
-
-                    if lag:
-                        pl.when(i >= lag)(go)
-                    else:
-                        go()
-            for z_stage, first in ticks:
-
-                @pl.when(lax.rem(i, 2) == 1)
-                def _(z_stage=z_stage, first=first):
-                    zstep(z_stage, first + i // 2)
+            between = (i + longer - 1) // longer * ((2 * longer - 1 - i) // longer)
+
+            @pl.loop(0, 1 + between)
+            def _(side_of):
+                produce(head((1 - 2 * side_of) * (longer - i)))
+
+            @pl.when(i < longer)
+            def _():
+                pass_on(stage, i, ticks)
+
+    def pass_on(stage, i, ticks):
+        for group in range(GROUPS):
+            for flow, (way, half, hops) in enumerate(flows):
+                lag = longer - hops
+
+                def go(group=group, flow=flow, way=way, half=half, hops=hops, lag=lag):
+                    step = i - lag
+
+                    @pl.when(step > 0)
+                    def _():
+                        rcopy(stage, group, flow, step - 1).wait_recv()
+                        where = piece_rows(head(way * (hops - step)), group)
+                        p[stage % 2, where, half_of(half)] = (
+                            p[stage % 2, where, half_of(half)].astype(jnp.float32)
+                            + slots[group, base[flow] + step - 1].astype(jnp.float32)
+                        ).astype(jnp.bfloat16)
+
+                    rcopy(stage, group, flow, step).start()
+
+                if lag:
+                    pl.when(i >= lag)(go)
+                else:
+                    go()
+        for z_stage, first in ticks:
+
+            @pl.when(lax.rem(i, 2) == 1)
+            def _(z_stage=z_stage, first=first):
+                zstep(z_stage, first + i // 2)
 
     def summed(stage, group):
         halves = [
@@ -341,14 +351,10 @@
 
     blocks = rows // BLOCK
 
-    def block_at(i):
-        farthest = lax.rem(h + nh // 2, nh) // (BLOCK // share)
-        away = (i + 1) // 2 * (1 - 2 * lax.rem(i, 2)) * (1 - 2 * lax.rem(h, 2))
-        return lax.rem(farthest + away + blocks, blocks)
-
-    def attend(stage, index, slab, mask, keys, moving):
-        lane = lax.broadcasted_iota(jnp.int32, (BLOCK, width), 1)
-        where = pl.ds(pl.multiple_of(index * BLOCK, BLOCK), BLOCK)
+    def attend(stage, chunk, slab, mask, keys, moving):
+        lane = lax.broadcasted_iota(jnp.int32, (share, width), 1)
+        index = chunk // (BLOCK // share)
+        where = share_rows(chunk)
         taken = pl.ds(pl.multiple_of(index * BLOCK, BLOCK), keys) if moving else pl.ds(0, keys)
         query = q[where, :]
         zero = jnp.zeros_like(query)
@@ -365,7 +371,7 @@
             preferred_element_type=jnp.float32,
         )
         mixed = mixed / totals
-        mixed = jnp.where(lane < HD, mixed[:BLOCK], mixed[BLOCK:]).astype(jnp.bfloat16)
+        mixed = jnp.where(lane < HD, mixed[:share], mixed[share:]).astype(jnp.bfloat16)
         low = stages[stage][0] + 3 * width
         p[stage % 2 if stage < 2 else 1, where, :] = contract_rows(
             mixed, wall[:, low : low + width]
@@ -447,8 +453,8 @@
     for o in (1, -1):
         side(eslab, o, 0).wait_recv()
 
-    def encode(i):
-        attend(0, block_at(i), eslab, listed_mask(enc_bias), 3 * rows, False)
+    def encode(chunk):
+        attend(0, chunk, eslab, listed_mask(enc_bias), 3 * rows, False)
 
     scattered(0, encode, ())
     zstep(1, z_steps)
@@ -500,8 +506,8 @@
     for move in (moves[3], moves[2], *passed):
         move.wait_recv()
 
-    def process(i):
-        attend(1, block_at(i), wslab, window_mask, 2 * REACH * rows + BLOCK, True)
+    def process(chunk):
+        attend(1, chunk, wslab, window_mask, 2 * REACH * rows + BLOCK, True)
 
     scattered(1, process, ((2, 1),))
 
@@ -516,9 +522,9 @@
     finish(1, state_rows, after_processor)
     zfinish(2)
 
-    def feed(i):
+    def feed(chunk):
         low = stages[2][0]
-        where = pl.ds(pl.multiple_of(block_at(i) * BLOCK, BLOCK), BLOCK)
+        where = share_rows(chunk)
         inner = jnp.dot(x[where, :], wall[:, low : low + ff], preferred_element_type=jnp.float32)
         hidden = (inner * 0.5 * (1.0 + lax.erf(inner * 0.5**0.5))).astype(jnp.bfloat16)
         p[0, where, :] = contract_rows(hidden, wall[:, low + ff : low + 2 * ff]).astype(jnp.bfloat16)
@@ -542,8 +548,8 @@
     for o in (1, -1):
         side(dslab, o, 8).wait_recv()
 
-    def decode(i):
-        attend(3, block_at(i), dslab, listed_mask(dec_bias), 3 * rows, False)
+    def decode(chunk):
+        attend(3, chunk, dslab, listed_mask(dec_bias), 3 * rows, False)
 
     scattered(3, decode, ())
     for group in range(GROUPS):

time: 192 us -> 191 us (level)
  no operation moved by 1% of the time
where the time goes in v5:
time: 191 us
  Pallas kernels  190 us (99%)
    pallas_call x1, Pallas kernels, per_device(): pl.pallas_call(functools.partial(kernel, nb, nh), out_shape=jax.ShapeDtyp...  190 us

profile of v5, /device:TPU:65, one launch (start us, length us, event | category | flops | bytes accessed | tf_op | source)
XLA Modules:
  0.0 191.3 jit_solution(1304862314903035487)
XLA Ops:
  0.0 189.7 %shard_map.145 = bf16[64,1024]{1,0:T(8,128)(2,1)} custom-call(bf16[512,1024]{1,0:T(8,128)(2,1)} %grid_ref.1, bf16[512,1024]{1,0:T(8,128)(2,1)} %mesh_ref.1, bf16[3,32,128]{2,1,0:T(8,128)(2,1)} %enc_in.1, bf16[32,128]{1,0:T(8,128)(2,1)} %bitcast.11, bf16[3,32,128]{2,1,0:T(8,128)(2,1)} %proc_in.1, bf16[32,128]{1,0:T(8,128)(2,1)} %bitcast.12, ...), custom_call_target="tpu_custom_call" | custom-call | tf_op jit(solution)/shard_map/pallas_call | solution.py:616
  189.7 1.6 copy.17
